TPU v7x, 32 devices: a whole 2x2x4 slice. The times are simulated.
32 devices in a mesh: data: 32 (over z, y, x, core).
Axes of the slice: x: 2, y: 2, z: 4, core: 2. Of those that a mesh axis runs over, the one named last changes fastest.
Arguments:
- tokens: bfloat16 [32768, 384], P('data')
- w_in: bfloat16 [384, 1536], replicated
- w_out: bfloat16 [1536, 384], replicated
- task_heads: bfloat16 [2, 384, 10], replicated
- labels: int32 [2, 32768], P(None, 'data')
- label_mask: int32 [2, 32768], P(None, 'data')
Outputs:
- output 1: float32 [2], replicated
- output 2: float32 [589824], P('data')
- output 3: float32 [589824], P('data')
All inputs are finite; a program needn't handle non-finite values.
Results may differ from a plain program's by a relative error of at most 0.0034077.
Values are sent between devices in bfloat16 or wider.
A program may use at most 1 GiB of HBM per device.

v0:
```python
import jax
import jax.numpy as jnp
from jax import lax
from jax.sharding import PartitionSpec as P

SOLVER_STEPS = 20


def device_grads(x_loc, w_in, w_out, task_heads, lab_loc, mask_loc):
    pre_act = jnp.dot(x_loc, w_in, preferred_element_type=jnp.float32)
    act_out, gelu_slope = jax.jvp(jax.nn.gelu, (pre_act,), (jnp.ones_like(pre_act),))
    act_bf = act_out.astype(jnp.bfloat16)
    residual = x_loc.astype(jnp.float32) + jnp.dot(act_bf, w_out, preferred_element_type=jnp.float32)
    z_bf = residual.astype(jnp.bfloat16)
    logits = jnp.einsum("bd,tdc->tbc", z_bf, task_heads, preferred_element_type=jnp.float32)
    soft_prob = jax.nn.softmax(logits, axis=-1)
    class_ids = jnp.arange(logits.shape[-1])
    onehot = (lab_loc[:, :, None] == class_ids).astype(jnp.float32)
    d_logit = (mask_loc[:, :, None].astype(jnp.float32) * (soft_prob - onehot)).astype(jnp.bfloat16)
    d_resid = jnp.einsum("tbc,tdc->tbd", d_logit, task_heads, preferred_element_type=jnp.float32).astype(jnp.bfloat16)
    grad_w_out = jnp.einsum("bf,tbd->tfd", act_bf, d_resid, preferred_element_type=jnp.float32)
    d_act = jnp.einsum("tbd,fd->tbf", d_resid, w_out, preferred_element_type=jnp.float32)
    d_pre = (d_act * gelu_slope[None]).astype(jnp.bfloat16)
    grad_w_in = jnp.einsum("bd,tbf->tdf", x_loc, d_pre, preferred_element_type=jnp.float32)
    return grad_w_in, grad_w_out


def gram_of(grad_rows):
    return jnp.einsum("tk,sk->ts", grad_rows, grad_rows, precision=lax.Precision.HIGHEST, preferred_element_type=jnp.float32)


def solve_weights(gram_mat):
    num_tasks = gram_mat.shape[0]
    step_scale = jnp.trace(gram_mat) / num_tasks

    def solver_step(step_idx, weights):
        pull_vec = (gram_mat * weights[None, :]).sum(axis=1)
        raised = weights * jnp.exp(-pull_vec / step_scale)
        return raised / raised.sum()

    init_weights = jnp.full((num_tasks,), 1.0 / num_tasks, jnp.float32)
    return lax.fori_loop(0, SOLVER_STEPS, solver_step, init_weights)


def solution(mesh):
    group_size = mesh.shape["data"]

    def local_step(x_loc, w_in, w_out, task_heads, lab_loc, mask_loc):
        num_tasks = task_heads.shape[0]
        label_count = lax.psum(mask_loc.sum(axis=1), "data")
        inv_count = 1.0 / jnp.maximum(label_count, 1).astype(jnp.float32)
        grad_w_in, grad_w_out = device_grads(x_loc, w_in, w_out, task_heads, lab_loc, mask_loc)
        shards = []
        for grad_full in (grad_w_in, grad_w_out):
            scaled = (grad_full.reshape(num_tasks, group_size, -1) * inv_count[:, None, None]).astype(jnp.bfloat16)
            arrived = lax.all_to_all(scaled, "data", 1, 1, tiled=True)
            shards.append(arrived.sum(axis=1, dtype=jnp.float32))
        gram_mat = lax.psum(gram_of(shards[0]) + gram_of(shards[1]), "data")
        weights = solve_weights(gram_mat)
        grad_in = (weights[:, None] * shards[0]).sum(axis=0)
        grad_out = (weights[:, None] * shards[1]).sum(axis=0)
        return weights, grad_in, grad_out

    return jax.shard_map(local_step, mesh=mesh, in_specs=(P("data", None), P(), P(), P(), P(None, "data"), P(None, "data")), out_specs=(P(), P("data"), P("data")), check_vma=False)
```

profile of v0, /device:TPU:0, one launch (start us, length us, event | category | flops | bytes accessed | tf_op | source)
XLA Modules:
  0.0 302.1 jit_solution(16143772871402776914)
XLA Ops:
  0.6 0.9 fusion.33
  1.9 7.9 %fusion.11 = (f32[1024,1536]{1,0:T(8,128)}, f32[1024,1536]{1,0:T(8,128)}) fusion(bf16[1024,384]{1,0:T(8,128)(2,1)} %param.8, bf16[384,1536]{1,0:T(8,128)(2,1)S(1)} %copy-done), kind=kOutput, calls=%fused_computation.18 | convolution fusion | flops 1233125376 | bytes 14548992 | tf_op jit(solution)/shard_map/dot_general | solution.py:10
  9.9 4.7 %fusion.19 = f32[2,1024,10]{1,2,0:T(8,128)S(1)} fusion(bf16[1536,384]{1,0:T(8,128)(2,1)S(1)} %copy-done.5, bf16[1024,384]{1,0:T(8,128)(2,1)} %param.8, bf16[2,384,10]{1,0,2:T(2,128)(2,1)S(1)} %copy-done.2, f32[1024,1536]{1,0:T(8,128)} %get-tuple-element.58), kind=kOutput, calls=%fused_computation.34 | convolution fusion | flops 1239023616 | bytes 8354816 | tf_op jit(solution)/shard_map/bd,tdc->tbc/dot_general | solution.py:15
  14.6 0.7 convolution_convert_fusion
  15.3 7.7 %convolution_bitcast_fusion.1 = f32[2,1536,384]{1,2,0:T(8,128)} fusion(bf16[2,1024,384]{2,1,0:T(8,128)(2,1)S(1)} %convolution_convert_fusion, f32[1024,1536]{1,0:T(8,128)} %get-tuple-element.58), kind=kOutput, calls=%fused_computation.25 | convolution fusion | flops 2430074880 | bytes 12582912 | tf_op jit(solution)/shard_map/bf,tbd->tfd/dot_general | solution.py:21
  23.0 6.1 %copy.33 = f32[2,1536,384]{2,1,0:T(8,128)} copy(f32[2,1536,384]{1,2,0:T(8,128)} %convolution_bitcast_fusion.1) | data formatting | bytes 9437184 | tf_op jit(solution)/shard_map/bf,tbd->tfd/transpose | solution.py:21
  29.0 5.2 %reshape.22 = f32[2,32,18432]{2,1,0:T(8,128)} reshape(f32[2,1536,384]{2,1,0:T(8,128)} %copy.33) | data formatting | bytes 9437184 | tf_op jit(solution)/shard_map/reshape | solution.py:55
  34.2 12.3 %convolution_bitcast_fusion = f32[2,384,1536]{1,2,0:T(8,128)} fusion(bf16[2,1024,384]{2,1,0:T(8,128)(2,1)S(1)} %convolution_convert_fusion, f32[1024,1536]{1,0:T(8,128)} %get-tuple-element.57, bf16[1536,384]{1,0:T(8,128)(2,1)} %param.10, bf16[1024,384]{1,0:T(8,128)(2,1)} %param.8), kind=kOutput, calls=%fused_computation.24 | convolution fusion | flops 4838129664 | bytes 14548992 | tf_op jit(solution)/shard_map/bd,tbf->tdf/dot_general | solution.py:24
  46.5 6.1 %copy.30 = f32[2,384,1536]{2,1,0:T(8,128)} copy(f32[2,384,1536]{1,2,0:T(8,128)} %convolution_bitcast_fusion) | data formatting | bytes 9437184 | tf_op jit(solution)/shard_map/bd,tbf->tdf/transpose | solution.py:24
  52.5 6.2 %reshape.21 = f32[2,32,18432]{2,1,0:T(8,128)} reshape(f32[2,384,1536]{2,1,0:T(8,128)} %copy.30) | data formatting | bytes 9437184 | tf_op jit(solution)/shard_map/reshape | solution.py:55
  58.7 41.9 %psum.14 = s32[2]{0:T(128)S(1)} all-reduce(s32[2]{0:T(128)S(1)} %get-tuple-element.53), channel_id=1, replica_groups=mesh['data'=32] {'data'}, use_global_device_ids=true, to_apply=%region_3.0 | all-reduce | flops 2 | bytes 16 | tf_op jit(solution)/shard_map/psum | solution.py:50
  100.7 5.8 %multiply_convert_fusion.2 = (bf16[2,32,18432]{2,1,0:T(8,128)(2,1)}, bf16[2,32,18432]{2,1,0:T(8,128)(2,1)S(1)}) fusion(f32[2,32,18432]{2,1,0:T(8,128)} %reshape.22, f32[2]{0:T(128)S(1)} %convert_divide_fusion, f32[2,32,18432]{2,1,0:T(8,128)} %reshape.21), kind=kLoop, calls=%fused_computation.21 | loop fusion | flops 4718592 | bytes 14155784 | tf_op jit(solution)/shard_map/convert_element_type | solution.py:55
  106.5 3.8 %copy.31 = bf16[2,32,18432]{2,0,1:T(2,128)(2,1)} copy(bf16[2,32,18432]{2,1,0:T(8,128)(2,1)S(1)} %get-tuple-element.56) | data formatting | bytes 4718592 | tf_op jit(solution)/shard_map/convert_element_type | solution.py:55
  110.3 4.7 %all-to-all-start = ((bf16[2,32,18432]{2,0,1:T(2,128)(2,1)}), bf16[2,32,18432]{2,0,1:T(2,128)(2,1)S(1)}, u32[]{:S(2)}, u32[]{:S(2)}) async-start(bf16[2,32,18432]{2,0,1:T(2,128)(2,1)} %copy.31), calls=%async_computation | async-start | bytes 4718592 | tf_op jit(solution)/shard_map/all_to_all | solution.py:56
  115.0 5.5 %copy.34 = bf16[2,32,18432]{2,0,1:T(2,128)(2,1)} copy(bf16[2,32,18432]{2,1,0:T(8,128)(2,1)} %get-tuple-element.55) | data formatting | bytes 4718592 | tf_op jit(solution)/shard_map/convert_element_type | solution.py:55
  120.5 48.9 %all-to-all-done = bf16[2,32,18432]{2,0,1:T(2,128)(2,1)S(1)} async-done(((bf16[2,32,18432]{2,0,1:T(2,128)(2,1)}), bf16[2,32,18432]{2,0,1:T(2,128)(2,1)S(1)}, u32[]{:S(2)}, u32[]{:S(2)}) %all-to-all-start) | async-done | bytes 2359328 | tf_op jit(solution)/shard_map/all_to_all | solution.py:56
  169.4 3.7 %all-to-all-start.1 = ((bf16[2,32,18432]{2,0,1:T(2,128)(2,1)}), bf16[2,32,18432]{2,0,1:T(2,128)(2,1)}, u32[]{:S(2)}, u32[]{:S(2)}) async-start(bf16[2,32,18432]{2,0,1:T(2,128)(2,1)} %copy.34), calls=%async_computation.1 | async-start | bytes 4718592 | tf_op jit(solution)/shard_map/all_to_all | solution.py:56
  173.1 1.9 convert_reduce_fusion.1
  175.0 0.7 copy-done.1
  175.7 1.4 fusion.34
  177.1 50.6 %all-to-all-done.1 = bf16[2,32,18432]{2,0,1:T(2,128)(2,1)} async-done(((bf16[2,32,18432]{2,0,1:T(2,128)(2,1)}), bf16[2,32,18432]{2,0,1:T(2,128)(2,1)}, u32[]{:S(2)}, u32[]{:S(2)}) %all-to-all-start.1) | async-done | bytes 2359328 | tf_op jit(solution)/shard_map/all_to_all | solution.py:56
  227.7 3.6 %convert_reduce_fusion = f32[2,18432]{1,0:T(2,128)S(1)} fusion(bf16[2,32,18432]{2,0,1:T(2,128)(2,1)} %all-to-all-done.1), kind=kLoop, calls=%fused_computation.20 | loop fusion | flops 2322432 | bytes 2506752 | tf_op jit(solution)/shard_map/reduce_sum | solution.py:57
  231.3 1.4 convolution_add_fusion
  232.7 37.8 %psum.15 = f32[2,2]{1,0:T(2,128)S(1)} all-reduce(f32[2,2]{1,0:T(2,128)S(1)} %convolution_add_fusion), channel_id=1, replica_groups=mesh['data'=32] {'data'}, use_global_device_ids=true, to_apply=%region_6.0 | all-reduce | flops 4 | bytes 32 | tf_op jit(solution)/shard_map/psum | solution.py:58
  271.7 28.4 %while.11 = (s32[]{:T(128)}, f32[2]{0:T(128)S(1)}, f32[2,2]{1,0:T(2,128)S(1)}, f32[]{:T(128)}, s32[]{:T(128)}, /*index=5*/s32[]{:T(128)}) while((s32[]{:T(128)}, f32[2]{0:T(128)S(1)}, f32[2,2]{1,0:T(2,128)S(1)}, f32[]{:T(128)}, s32[]{:T(128)}, /*index=5*/s32[]{:T(128)}) %tuple.33), condition=%wide.region_11.12_spmd.clone, body=%wide.region_8.11_spmd.clone.sunk | while | flops 22 | bytes 180 | solution.py:42
  271.9 0.6 fusion.46
  272.5 0.6 broadcast_divide_fusion.2
  273.3 0.6 fusion.46
  273.9 0.6 broadcast_divide_fusion.2
  275.3 0.6 broadcast_divide_fusion.2
  276.8 0.6 broadcast_divide_fusion.2
  278.2 0.6 broadcast_divide_fusion.2
  279.6 0.6 broadcast_divide_fusion.2
  281.0 0.6 broadcast_divide_fusion.2
  282.4 0.6 broadcast_divide_fusion.2
  283.8 0.6 broadcast_divide_fusion.2
  285.3 0.6 broadcast_divide_fusion.2
  286.7 0.6 broadcast_divide_fusion.2
  288.1 0.6 broadcast_divide_fusion.2
  289.5 0.6 broadcast_divide_fusion.2
  290.9 0.6 broadcast_divide_fusion.2
  292.4 0.6 broadcast_divide_fusion.2
  293.8 0.6 broadcast_divide_fusion.2
  295.2 0.6 broadcast_divide_fusion.2
  296.6 0.6 broadcast_divide_fusion.2
  298.0 0.6 broadcast_divide_fusion.2
  299.5 0.6 broadcast_divide_fusion.2
  300.1 2.0 multiply_reduce_fusion.1
  (72 shorter events, 14.6 us)
Async XLA Ops:
  0.6 1.3 copy-start
  1.9 7.9 %copy-start.2 = (bf16[2,384,10]{1,0,2:T(2,128)(2,1)S(1)}, bf16[2,384,10]{1,0,2:T(2,128)(2,1)}, u32[]{:S(2)}) copy-start(bf16[2,384,10]{1,0,2:T(2,128)(2,1)} %param.11) | copy-start | bytes 46084
  1.9 7.9 %copy-start.5 = (bf16[1536,384]{1,0:T(8,128)(2,1)S(1)}, bf16[1536,384]{1,0:T(8,128)(2,1)}, u32[]{:S(2)}) copy-start(bf16[1536,384]{1,0:T(8,128)(2,1)} %param.10) | copy-start | bytes 3538948
  9.9 4.7 %copy-start.4 = (s32[2,1024]{1,0:T(2,128)S(1)}, s32[2,1024]{1,0:T(2,128)}, u32[]{:S(2)}) copy-start(s32[2,1024]{1,0:T(2,128)} %param.12) | copy-start | bytes 24580
  110.3 59.1 %all-to-all-start = ((bf16[2,32,18432]{2,0,1:T(2,128)(2,1)}), bf16[2,32,18432]{2,0,1:T(2,128)(2,1)S(1)}, u32[]{:S(2)}, u32[]{:S(2)}) async-start(bf16[2,32,18432]{2,0,1:T(2,128)(2,1)} %copy.31), calls=%async_computation | async-start | bytes 4718592 | tf_op jit(solution)/shard_map/all_to_all | solution.py:56
  169.4 58.2 %all-to-all-start.1 = ((bf16[2,32,18432]{2,0,1:T(2,128)(2,1)}), bf16[2,32,18432]{2,0,1:T(2,128)(2,1)}, u32[]{:S(2)}, u32[]{:S(2)}) async-start(bf16[2,32,18432]{2,0,1:T(2,128)(2,1)} %copy.34), calls=%async_computation.1 | async-start | bytes 4718592 | tf_op jit(solution)/shard_map/all_to_all | solution.py:56
  175.0 0.7 copy-start.1
  300.1 2.0 copy-start.3
where the time goes:
time: 304 us; the launch traced here: 302 us
  waiting for transfers between devices  99.5 us (33%)
  blocking collectives  79.7 us (26%)
  other arithmetic  42.6 us (14%)
  matrix products  36 us (12%)
  local copies, waits for them, and re-layouts  33.9 us (11%)
  starting transfers between devices  8.4 us (3%)
    all_to_all x2, waiting for transfers between devices, local_step(): arrived = lax.all_to_all(scaled, 'data', 1, 1, tiled=True)  99.5 us
    psum x1, blocking collectives, local_step(): label_count = lax.psum(mask_loc.sum(axis=1), 'data')  41.9 us
    psum x1, blocking collectives, local_step(): gram_mat = lax.psum(gram_of(shards[0]) + gram_of(shards[1]), 'data')  37.8 us
    div x20, other arithmetic, solver_step(): return raised / raised.sum()  13 us
    reduce_sum x20, other arithmetic, solver_step(): return raised / raised.sum()  12.4 us
    dot_general x1, matrix products, device_grads(): jnp.einsum('bd,tbf->tdf', x_loc, d_pre, preferred_element_type=jnp.float32)  12.3 us
    reshape x2, local copies, waits for them, and re-layouts, local_step(): grad_full.reshape(num_tasks, group_size, -1) * inv_count[:, None, None]  11.4 us
    convert_element_type x2, local copies, waits for them, and re-layouts, local_step(): (grad_full.reshape(num_tasks, group_size, -1) * inv_count[:, None, None])...  9.32 us
  transfers between devices with their start and end apart: 2, of which 2 were waited for; matrix products, arithmetic and copies ran while one was open for 3% of the time, Pallas kernels for 0%

commit v1 on v0

v1 whole, which is shorter than its diff:
```python
import functools

import jax
import jax.numpy as jnp
import numpy as np
from jax import lax
from jax.experimental import pallas as pl
from jax.experimental.pallas import tpu as pltpu
from jax.sharding import PartitionSpec as P

SOLVER_STEPS = 20
DEVICES = 32
DIM, HID, TOK, CLS = 384, 1536, 1024, 10
CHUNKS, TASKS = 3, 2
F32, BF16 = jnp.float32, jnp.bfloat16
GELU_C = 0.7978845608028654
GELU_A = 0.044715
PAIRS = ((0, 1), (1, 0), (1, 1))


def row_order():
    order = []
    for x in range(2):
        for c in range(2):
            for y in range(2):
                own = [8 * z + 4 * y + 2 * x + c for z in range(4)]
                for o in own:
                    order += [12 * o + i for i in range(8)]
                for o in own:
                    order += [12 * o + i for i in range(8, 12)]
    return np.array(order)


def select_matrix():
    mat = np.zeros((DIM, DIM), np.float32)
    mat[np.arange(DIM), row_order()] = 1.0
    return mat


def dot(a, b, dims):
    return lax.dot_general(a, b, (dims, ((), ())), preferred_element_type=F32)


def kernel(x_ref, w1_ref, w2_ref, heads_ref, lab_ref, mask_ref, sel_ref,
           weights_ref, gin_ref, gout_ref,
           act_ref, slope_ref, xsel_ref, dzt_ref, dz_ref, zt_ref,
           a1_send, b1_send, a1_recv, b1_recv,
           a2_own, b2_own, a2_send, b2_send, a2_recv, b2_recv,
           a3_send, b3_send, a3_recv, b3_recv, ga_ref, gb_ref,
           cnt_ref, gram_ref,
           s1_ssem, s1_rsem, s2_ssem, s2_rsem, s3_ssem, s3_rsem,
           cnt_ssem, cnt_rsem, gram_ssem, gram_rsem):
    me = lax.axis_index("data")
    core = lax.rem(me, 2)
    px = lax.rem(me // 2, 2)
    py = lax.rem(me // 4, 2)
    pz = me // 8

    def device(z, y, x, c):
        return (z * 8 + y * 4 + x * 2 + c,)

    def flip(v, d):
        return lax.rem(v + d, 2)

    def remote(src, dst, ssem, rsem, dev):
        return pltpu.make_async_remote_copy(src_ref=src, dst_ref=dst, send_sem=ssem, recv_sem=rsem,
                                            device_id=dev, device_id_type=pl.DeviceIdType.MESH)

    barrier = pltpu.get_barrier_semaphore()

    @pl.loop(1, DEVICES)
    def _(d):
        pl.semaphore_signal(barrier, inc=1, device_id=(lax.rem(me + d, DEVICES),),
                            device_id_type=pl.DeviceIdType.MESH)

    def row_copy(buf, ssem, rsem, d, slot):
        return remote(buf.at[slot], buf.at[slot], ssem.at[d], rsem.at[d], (lax.rem(me + d, DEVICES),))

    def row_start(buf, ssem, rsem):
        @pl.loop(1, DEVICES)
        def _(d):
            row_copy(buf, ssem, rsem, d, me).start()

    def row_wait(buf, ssem, rsem):
        @pl.loop(1, DEVICES)
        def _(d):
            row_copy(buf, ssem, rsem, d, lax.rem(me + (DEVICES - d), DEVICES)).wait_recv()

    def row_drain(buf, ssem, rsem):
        @pl.loop(1, DEVICES)
        def _(d):
            row_copy(buf, ssem, rsem, d, me).wait_send()

    lane = lax.broadcasted_iota(jnp.int32, (1, 128), 1)

    def lane_pick(row, k):
        return jnp.sum(jnp.where(lane == k, row, 0.0), axis=1, keepdims=True)

    counts = jnp.sum(mask_ref[...].astype(F32), axis=1, keepdims=True)
    cnt_ref[me] = jnp.where(lane == 0, counts[0:1], jnp.where(lane == 1, counts[1:2], 0.0))

    xt = jnp.transpose(x_ref[...])
    xsel_ref[...] = dot(sel_ref[...], xt, ((1,), (0,))).astype(BF16)
    zt_ref[...] = xt.astype(F32)

    @pl.loop(0, HID // 384)
    def _(i):
        cols = pl.ds(pl.multiple_of(i * 384, 384), 384)
        pre = dot(w1_ref[:, cols], x_ref[...], ((0,), (1,)))
        sq = pre * pre
        th = jnp.tanh(pre * (GELU_C + (GELU_C * GELU_A) * sq))
        cdf = 0.5 * (1.0 + th)
        act = (pre * cdf).astype(BF16)
        act_ref[pl.ds(pl.multiple_of(i * 8, 8), 8)] = act.reshape(8, CHUNKS, 16, TOK)
        slope_ref[cols, :] = cdf + 0.5 * pre * (1.0 - th * th) * (GELU_C + (3.0 * GELU_C * GELU_A) * sq)
        zt_ref[...] += dot(w2_ref[cols, :], act, ((0,), (0,)))

    pl.semaphore_wait(barrier, DEVICES - 1)
    row_start(cnt_ref, cnt_ssem, cnt_rsem)

    zt = zt_ref[...].astype(BF16)
    cls = lax.broadcasted_iota(jnp.int32, (CLS, TOK), 0)
    for t in range(TASKS):
        head = heads_ref[t]
        logits = dot(head, zt, ((0,), (0,)))
        ex = jnp.exp(logits - jnp.max(logits, axis=0, keepdims=True))
        prob = ex / jnp.sum(ex, axis=0, keepdims=True)
        onehot = jnp.where(lab_ref[t:t + 1, :] == cls, 1.0, 0.0)
        err = (mask_ref[t:t + 1, :].astype(F32) * (prob - onehot)).astype(BF16)
        dzt = dot(head, err, ((1,), (0,))).astype(BF16)
        dzt_ref[t] = dzt
        dz_ref[:, t * DIM:(t + 1) * DIM] = jnp.transpose(dzt)

    row_wait(cnt_ref, cnt_ssem, cnt_rsem)
    total = jnp.sum(cnt_ref[...], axis=0)
    inv = [1.0 / jnp.maximum(lane_pick(total, t), 1.0) for t in range(TASKS)]

    def compute_b(k):
        rows = [act_ref[8 * z + 4 * y + 2 * x + c, k]
                for y in range(2) for c in range(2) for z in range(4) for x in range(2)]
        part = dot(jnp.concatenate(rows, axis=0), dz_ref[...], ((1,), (0,)))
        for t in range(TASKS):
            b1_send[k, t] = (part[:, t * DIM:(t + 1) * DIM] * inv[t]).astype(BF16).reshape(4, 128, DIM)

    def compute_a(k, t):
        rows = slice(512 * k, 512 * (k + 1))
        back = dot(w2_ref[rows, :], dzt_ref[t], ((1,), (0,)))
        dpre = (back * slope_ref[rows, :]).astype(BF16)
        part = dot(xsel_ref[...], dpre, ((1,), (1,)))
        a1_send[k, t] = (part * inv[t]).astype(BF16).reshape(4, 96, 512)

    def s1_copy(color, k, t, p):
        dn, dc = PAIRS[p]
        c = flip(core, dc)
        if color == 0:
            x = flip(px, dn)
            return remote(a1_send.at[k, t, x * 2 + c], a1_recv.at[k, t, p],
                          s1_ssem.at[color, k, t, p], s1_rsem.at[color, k, t, p], device(pz, py, x, c))
        y = flip(py, dn)
        return remote(b1_send.at[k, t, y * 2 + c], b1_recv.at[k, t, p],
                      s1_ssem.at[color, k, t, p], s1_rsem.at[color, k, t, p], device(pz, y, px, c))

    def s2_copy(color, k, t):
        if color == 0:
            return remote(a2_send.at[k, t], a2_recv.at[k, t], s2_ssem.at[color, k, t], s2_rsem.at[color, k, t],
                          device(pz, flip(py, 1), px, core))
        return remote(b2_send.at[k, t], b2_recv.at[k, t], s2_ssem.at[color, k, t], s2_rsem.at[color, k, t],
                      device(pz, py, flip(px, 1), core))

    def s3_copy(color, k, t, d):
        z = lax.rem(pz + d, 4)
        send, recv = (a3_send, a3_recv) if color == 0 else (b3_send, b3_recv)
        return remote(send.at[k, t, z], recv.at[k, t, d - 1], s3_ssem.at[color, k, t, d - 1],
                      s3_rsem.at[color, k, t, d - 1], device(z, py, px, core))

    def s1_start(color, k, t):
        for p in (2, 1, 0):
            s1_copy(color, k, t, p).start()

    def s1_finish(color, k, t):
        for p in range(3):
            s1_copy(color, k, t, p).wait_recv()
        if color == 0:
            tot = a1_send[k, t, px * 2 + core].astype(F32)
            for p in range(3):
                tot = tot + a1_recv[k, t, p].astype(F32)
            first, second = tot[0:48], tot[48:96]
            keep = py == 0
            a2_own[k, t] = jnp.where(keep, first, second)
            a2_send[k, t] = jnp.where(keep, second, first)
        else:
            tot = b1_send[k, t, py * 2 + core].astype(F32)
            for p in range(3):
                tot = tot + b1_recv[k, t, p].astype(F32)
            tot = tot.reshape(4, 2, 16, DIM)
            keep = px == 0
            b2_own[k, t] = jnp.where(keep, tot[:, 0], tot[:, 1])
            b2_send[k, t] = jnp.where(keep, tot[:, 1], tot[:, 0])
        s2_copy(color, k, t).start()

    def s2_finish(color, k, t):
        s2_copy(color, k, t).wait_recv()
        if color == 0:
            tot = (a2_own[k, t] + a2_recv[k, t]).reshape(6, 8, 512)
            for z in range(4):
                a3_send[k, t, z, 0] = tot[z]
                a3_send[k, t, z, 1] = tot[4 + z // 2]
        else:
            b3_send[k, t] = b2_own[k, t] + b2_recv[k, t]
        for d in (2, 1, 3):
            s3_copy(color, k, t, d).start()

    def s3_finish(color, k, t):
        for d in range(1, 4):
            s3_copy(color, k, t, d).wait_recv()
        if color == 0:
            ga_ref[k, t] = (a3_send[k, t, pz] + a3_recv[k, t, 0]) + (a3_recv[k, t, 1] + a3_recv[k, t, 2])
        else:
            gb_ref[k, t] = (b3_send[k, t, pz] + b3_recv[k, t, 0]) + (b3_recv[k, t, 1] + b3_recv[k, t, 2])

    subs = [(k, t) for k in range(CHUNKS) for t in range(TASKS)]

    compute_b(0)
    s1_start(1, 0, 0)
    compute_a(0, 0)
    s1_start(0, 0, 0)
    s1_start(1, 0, 1)
    compute_a(0, 1)
    s1_start(0, 0, 1)
    compute_b(1)
    compute_a(1, 0)
    for n, (k, t) in enumerate(subs):
        for color in (1, 0):
            s1_finish(color, k, t)
        if n + 2 < len(subs):
            for color in (1, 0):
                s1_start(color, *subs[n + 2])
        if n >= 1:
            for color in (1, 0):
                s2_finish(color, *subs[n - 1])
        if n + 3 < len(subs):
            nk, nt = subs[n + 3]
            if nt == 0:
                compute_b(nk)
            compute_a(nk, nt)
        if n >= 3:
            for color in (1, 0):
                s3_finish(color, *subs[n - 3])
    for color in (1, 0):
        s2_finish(color, *subs[5])
    for n in (3, 4, 5):
        for color in (1, 0):
            s3_finish(color, *subs[n])

    half = lax.broadcasted_iota(jnp.int32, (8, 512), 0) // 4 == lax.rem(pz, 2)

    def own_rows(k, t):
        return ga_ref[k, t, 0], jnp.where(half, ga_ref[k, t, 1], 0.0)

    sums = [jnp.zeros((8, 128), F32)] * 3
    for k in range(CHUNKS):
        tops = [own_rows(k, t) for t in range(TASKS)]
        lows = [gb_ref[k, t] for t in range(TASKS)]
        for q, (s, t) in enumerate(((0, 0), (0, 1), (1, 1))):
            prod = tops[s][0] * tops[t][0] + tops[s][1] * tops[t][1]
            for j in range(4):
                sums[q] = sums[q] + prod[:, 128 * j:128 * (j + 1)]
            prod = lows[s] * lows[t]
            prod = prod[0:8] + prod[8:16]
            for j in range(3):
                sums[q] = sums[q] + prod[:, 128 * j:128 * (j + 1)]
    row = jnp.zeros((1, 128), F32)
    for q in range(3):
        one = jnp.sum(jnp.sum(sums[q], axis=0, keepdims=True), axis=1, keepdims=True)
        row = jnp.where(lane == q, one, row)
    gram_ref[me] = row
    row_start(gram_ref, gram_ssem, gram_rsem)
    row_wait(gram_ref, gram_ssem, gram_rsem)
    total = jnp.sum(gram_ref[...], axis=0)
    m00, m01, m11 = [jnp.broadcast_to(lane_pick(total, q), (1, 128)) for q in range(3)]
    scale = (m00 + m11) / 2.0
    w0 = jnp.full((1, 128), 0.5, F32)
    w1 = w0
    for _ in range(SOLVER_STEPS):
        r0 = w0 * jnp.exp(-(m00 * w0 + m01 * w1) / scale)
        r1 = w1 * jnp.exp(-(m01 * w0 + m11 * w1) / scale)
        norm = r0 + r1
        w0 = r0 / norm
        w1 = r1 / norm
    weights_ref[...] = jnp.where(lane == 0, w0, w1)

    for k in range(CHUNKS):
        mix = w0[:, 0:1] * gb_ref[k, 0] + w1[:, 0:1] * gb_ref[k, 1]
        for j in range(3):
            gout_ref[pl.ds(48 * k + j, 16, stride=3), :] = mix[:, 128 * j:128 * (j + 1)]
        top = w0[:, 0:1] * ga_ref[k, 0, 0] + w1[:, 0:1] * ga_ref[k, 1, 0]
        low = w0[:, 0:1] * ga_ref[k, 0, 1] + w1[:, 0:1] * ga_ref[k, 1, 1]
        low = jnp.where(lax.rem(pz, 2) == 0, low[0:4], low[4:8])
        for j in range(4):
            gin_ref[pl.ds(4 * k + j, 8, stride=12), :] = top[:, 128 * j:128 * (j + 1)]
            gin_ref[pl.ds(96 + 4 * k + j, 4, stride=12), :] = low[:, 128 * j:128 * (j + 1)]

    row_drain(cnt_ref, cnt_ssem, cnt_rsem)
    row_drain(gram_ref, gram_ssem, gram_rsem)
    for k, t in subs:
        for color in (0, 1):
            for p in range(3):
                s1_copy(color, k, t, p).wait_send()
                s3_copy(color, k, t, p + 1).wait_send()
            s2_copy(color, k, t).wait_send()


def solution(mesh):
    sel = select_matrix()

    def local_step(x_loc, w_in, w_out, task_heads, lab_loc, mask_loc):
        vmem = pl.BlockSpec(memory_space=pltpu.VMEM)
        sub = (CHUNKS, TASKS)
        dma = pltpu.SemaphoreType.DMA
        scratch = [
            pltpu.VMEM((32, CHUNKS, 16, TOK), BF16),
            pltpu.VMEM((HID, TOK), F32),
            pltpu.VMEM((DIM, TOK), BF16),
            pltpu.VMEM((TASKS, DIM, TOK), BF16),
            pltpu.VMEM((TOK, TASKS * DIM), BF16),
            pltpu.VMEM((DIM, TOK), F32),
            pltpu.VMEM(sub + (4, 96, 512), BF16),
            pltpu.VMEM(sub + (4, 128, DIM), BF16),
            pltpu.VMEM(sub + (3, 96, 512), BF16),
            pltpu.VMEM(sub + (3, 128, DIM), BF16),
            pltpu.VMEM(sub + (48, 512), F32),
            pltpu.VMEM(sub + (4, 16, DIM), F32),
            pltpu.VMEM(sub + (48, 512), F32),
            pltpu.VMEM(sub + (4, 16, DIM), F32),
            pltpu.VMEM(sub + (48, 512), F32),
            pltpu.VMEM(sub + (4, 16, DIM), F32),
            pltpu.VMEM(sub + (4, 2, 8, 512), F32),
            pltpu.VMEM(sub + (4, 16, DIM), F32),
            pltpu.VMEM(sub + (3, 2, 8, 512), F32),
            pltpu.VMEM(sub + (3, 16, DIM), F32),
            pltpu.VMEM(sub + (2, 8, 512), F32),
            pltpu.VMEM(sub + (16, DIM), F32),
            pltpu.VMEM((DEVICES, 1, 128), F32),
            pltpu.VMEM((DEVICES, 1, 128), F32),
            dma((2,) + sub + (3,)), dma((2,) + sub + (3,)),
            dma((2,) + sub), dma((2,) + sub),
            dma((2,) + sub + (3,)), dma((2,) + sub + (3,)),
            dma((DEVICES,)), dma((DEVICES,)), dma((DEVICES,)), dma((DEVICES,)),
        ]
        weights, grad_in, grad_out = pl.pallas_call(
            kernel,
            out_shape=[jax.ShapeDtypeStruct((1, 128), F32),
                       jax.ShapeDtypeStruct((144, 128), F32),
                       jax.ShapeDtypeStruct((144, 128), F32)],
            in_specs=[vmem] * 7,
            out_specs=[vmem] * 3,
            scratch_shapes=scratch,
            compiler_params=pltpu.CompilerParams(collective_id=0, has_side_effects=True,
                                                 vmem_limit_bytes=60 * 2 ** 20),
            name="step",
        )(x_loc, w_in, w_out, task_heads, lab_loc, mask_loc, jnp.asarray(sel, BF16))
        return weights[0, :2], grad_in.reshape(-1), grad_out.reshape(-1)

    return jax.shard_map(local_step, mesh=mesh,
                         in_specs=(P("data", None), P(), P(), P(), P(None, "data"), P(None, "data")),
                         out_specs=(P(), P("data"), P("data")), check_vma=False)
```

time: 304 us -> 84.2 us (0.28)
  waiting for transfers between devices: 99.5 us -> 0 us
  blocking collectives: 79.7 us -> 0 us
  Pallas kernels: 0 us -> 77.5 us
  other arithmetic: 42.6 us -> 0 us
  matrix products: 36 us -> 0 us
  local copies, waits for them, and re-layouts: 33.9 us -> 5.73 us
  starting transfers between devices: 8.4 us -> 0 us
    all_to_all x2 -> x0, waiting for transfers between devices: 99.5 us -> none  [local_step(): arrived = lax.all_to_all(scaled, 'data', 1, 1, tiled=True)]
    psum x2 -> x0, blocking collectives: 79.7 us -> none  [the longest x1 41.9 us: local_step(): label_count = lax.psum(mask_loc.sum(axis=1), 'data')]
    pallas_call x0 -> x1, Pallas kernels: none -> 77.5 us  [local_step(): pl.pallas_call(kernel, out_shape=[jax.ShapeDtypeStruct((1, 128), F32), ja...]
    dot_general x7 -> x0, matrix products: 36 us -> none  [the longest x1 12.3 us: device_grads(): jnp.einsum('bd,tbf->tdf', x_loc, d_pre, preferred_element_type=jnp.float32)]
    reduce_sum x45 -> x0, other arithmetic: 23.7 us -> none  [the longest x20 12.4 us: solver_step(): return raised / raised.sum()]
    div x21 -> x0, other arithmetic: 13 us -> none  [the longest x20 13 us: solver_step(): return raised / raised.sum()]
    transpose x2 -> x0, local copies, waits for them, and re-layouts: 12.1 us -> none  [the longest x1 6.06 us: device_grads(): jnp.einsum('bd,tbf->tdf', x_loc, d_pre, preferred_element_type=jnp.float32)]
    reshape x2 -> x0, local copies, waits for them, and re-layouts: 11.4 us -> none  [local_step(): grad_full.reshape(num_tasks, group_size, -1) * inv_count[:, None, None]]
  transfers between devices with their start and end apart: 2 -> 0, of which waited for: 2 -> 0; matrix products, arithmetic and copies ran while one was open for 3% -> 0% of each run, Pallas kernels for 0% -> 0%
where the time goes in v1:
time: 84.2 us; the launch traced here: 83.9 us
  Pallas kernels  77.5 us (92%)
  local copies, waits for them, and re-layouts  5.73 us (7%)
    pallas_call x1, Pallas kernels, local_step(): pl.pallas_call(kernel, out_shape=[jax.ShapeDtypeStruct((1, 128), F32), ja...  77.5 us
    unnamed x3, local copies, waits for them, and re-layouts  4.59 us

profile of v1, /device:TPU:0, one launch (start us, length us, event | category | flops | bytes accessed | tf_op | source)
XLA Modules:
  0.0 83.9 jit_solution(10862794659804861926)
XLA Ops:
  0.6 1.5 %copy.10.heads_ref = bf16[2,384,10]{2,1,0:T(8,128)(2,1)} copy(bf16[2,384,10]{1,0,2:T(2,128)(2,1)} %param.10) | data formatting | bytes 30720 | tf_op args[3]
  2.2 77.5 %step.1 = (f32[1,128]{1,0:T(1,128)}, f32[144,128]{1,0:T(8,128)}, f32[144,128]{1,0:T(8,128)}) custom-call(bf16[1024,384]{1,0:T(8,128)(2,1)} %x_ref.1, bf16[384,1536]{1,0:T(8,128)(2,1)} %w1_ref.1, bf16[1536,384]{1,0:T(8,128)(2,1)} %w2_ref.1, bf16[2,384,10]{2,1,0:T(8,128)(2,1)} %copy.10.heads_ref, s32[2,1024]{1,0:T(2,128)} %lab_ref.1, s32[2,1024]{1,0:T(2,128)} %mask_ref.1, ...), custom_call_target="tpu_custom_call" | custom-call | tf_op jit(solution)/shard_map/step/pallas_call | solution.py:350
  79.7 1.1 %slice_bitcast_fusion = f32[2]{0:T(128)} fusion(f32[1,128]{1,0:T(1,128)} %get-tuple-element.6), kind=kLoop, calls=%fused_computation | loop fusion | bytes 16 | tf_op jit(solution)/shard_map/squeeze | solution.py:362
  80.8 1.5 %copy.13 = f32[18432]{0:T(1024)} copy(f32[18432]{0:T(1024)} %bitcast.5) | data formatting | bytes 147456
  82.4 1.5 %copy.14 = f32[18432]{0:T(1024)} copy(f32[18432]{0:T(1024)} %bitcast.4) | data formatting | bytes 147456

commit v2 on v0

v2 whole, which is shorter than its diff:
```python
import contextlib

import jax
import jax.numpy as jnp
import numpy as np
from jax import lax
from jax.experimental import pallas as pl
from jax.experimental.pallas import tpu as pltpu
from jax.sharding import PartitionSpec as P

SOLVER_STEPS = 20
DEVICES = 32
DIM, HID, TOK, CLS = 384, 1536, 1024, 10
CHUNKS, TASKS = 3, 2
F32, BF16 = jnp.float32, jnp.bfloat16
GELU_C = 0.7978845608028654
GELU_A = 0.044715
PAIRS = ((0, 1), (1, 0), (1, 1))

PIECES = (((0, 0, 0), (0, 0, 1), (0, 1, 0), (0, 2, 0)),
          ((1, 0, 0), (1, 1, 0), (1, 2, 0), (1, 2, 1)),
          ((1, 0, 1), (1, 1, 1), (0, 1, 1), (0, 2, 1)))
ROUTE = {piece: (r, n) for r, pieces in enumerate(PIECES) for n, piece in enumerate(pieces)}
COLS = (512, DIM)
PLANE = (96, 128)
TILE = ((2, 8), (16,))


def no_scope(name):
    return contextlib.nullcontext()


scope = no_scope


def owner(z, y, x, c):
    return 8 * z + 4 * y + 2 * x + c


def tiles(owners):
    return [12 * o + i for o in owners for i in range(8)] + [12 * o + i for o in owners for i in range(8, 12)]


def row_orders():
    two = range(2)
    first = [r for x in two for c in two for y in two for r in tiles([owner(z, y, x, c) for z in range(4)])]
    third = [r for zl in two for c in two for y in two for x in two
             for r in tiles([owner(2 * zh + zl, y, x, c) for zh in two])]
    return first, third


def block_orders():
    two = range(2)
    second = [owner(z, y, x, c) for y in two for c in two for x in two for z in range(4)]
    third = [owner(2 * zh + zl, y, x, c) for zl in two for c in two for y in two for x in two for zh in two]
    return second, third


def select_matrices():
    mat = np.zeros((2, DIM, DIM), np.float32)
    for m, order in zip(mat, row_orders()):
        m[np.arange(DIM), np.array(order)] = 1.0
    return mat


def scoped(f):
    def call(*args):
        with scope("_".join([f.__name__, *map(str, args)])):
            return f(*args)
    return call


def dot(a, b, dims):
    return lax.dot_general(a, b, (dims, ((), ())), preferred_element_type=F32)


def kernel(x_hbm, w1_hbm, w2_hbm, heads_hbm, lab_hbm, mask_hbm, sel_hbm,
           gin_hbm, gout_hbm, gram_hbm,
           x_ref, w1_ref, w2_ref, heads_ref, lab_ref, mask_ref, sel_ref,
           gin_ref, gout_ref, gram_out,
           xt_ref, act_ref, slope_ref, xsel_ref, dzt_ref, dz_ref,
           a1_send, b1_send, a1_recv, b1_recv,
           a2_send, b2_send, a2_recv, b2_recv,
           a3_send, b3_send, a3_recv, b3_recv,
           ca2_send, cb2_send, ca2_recv, cb2_recv,
           ca3_send, cb3_send, ca3_recv, cb3_recv,
           cnt_ref, gram_ref,
           in_sem, out_sem, s1_rsem, s2_rsem, s3_rsem, ssem,
           cnt_ssem, cnt_rsem, gram_ssem, gram_rsem):
    me = lax.axis_index("data")
    core = lax.rem(me, 2)
    px = lax.rem(me // 2, 2)
    py = lax.rem(me // 4, 2)
    pz = me // 8
    zl, zh = lax.rem(pz, 2), pz // 2

    def device(z, y, x, c):
        return (owner(z, y, x, c),)

    def flip(v, d):
        return lax.rem(v + d, 2)

    def remote(src, dst, ssem, rsem, dev):
        return pltpu.make_async_remote_copy(src_ref=src, dst_ref=dst, send_sem=ssem, recv_sem=rsem,
                                            device_id=dev, device_id_type=pl.DeviceIdType.MESH)

    loads = {name: pltpu.make_async_copy(src, dst, in_sem.at[i]) for i, (name, src, dst) in enumerate((
        ("mask", mask_hbm, mask_ref), ("x", x_hbm, x_ref), ("w1", w1_hbm, w1_ref), ("w2", w2_hbm, w2_ref),
        ("heads", heads_hbm, heads_ref), ("lab", lab_hbm, lab_ref), ("sel", sel_hbm, sel_ref)))}
    for load in loads.values():
        load.start()

    barrier = pltpu.get_barrier_semaphore()

    @pl.loop(1, DEVICES)
    def _(d):
        pl.semaphore_signal(barrier, inc=1, device_id=(lax.rem(me + d, DEVICES),),
                            device_id_type=pl.DeviceIdType.MESH)

    def row_copy(buf, ssem, rsem, d):
        return remote(buf.at[me], buf.at[me], ssem, rsem, (lax.rem(me + d, DEVICES),))

    def row_start(buf, ssem, rsem):
        @pl.loop(1, DEVICES)
        def _(d):
            row_copy(buf, ssem, rsem, d).start()

    def row_all(buf, ssem, rsem):
        rows = buf.at[pl.ds(0, DEVICES - 1)]
        return remote(rows, rows, ssem, rsem, (lax.rem(me + 1, DEVICES),))

    lane = lax.broadcasted_iota(jnp.int32, (1, 128), 1)

    def lane_pick(row, k):
        return jnp.sum(jnp.where(lane == k, row, 0.0), axis=1, keepdims=True)

    loads["mask"].wait()
    counts = jnp.sum(mask_ref[...].astype(F32), axis=1, keepdims=True)
    cnt_ref[me] = jnp.where(lane == 0, counts[0:1], jnp.where(lane == 1, counts[1:2], 0.0))

    def forward(i):
        cols = slice(i * 384, (i + 1) * 384)
        pre = dot(w1_ref[:, cols], xt_ref[...], ((0,), (0,)))
        sq = pre * pre
        cdf = 0.5 + 0.5 * jnp.tanh(pre * (GELU_C + (GELU_C * GELU_A) * sq))
        act = pre * cdf
        act_ref[8 * i:8 * (i + 1)] = act.astype(BF16).reshape(8, CHUNKS, 16, TOK)
        slope_ref[cols, :] = cdf + act * (1.0 - cdf) * (2.0 * GELU_C + (6.0 * GELU_C * GELU_A) * sq)

    with scope("xt"):
        loads["x"].wait()
        xt_ref[...] = jnp.transpose(x_ref[...])
    with scope("fwd"):
        loads["w1"].wait()
        forward(0)
        forward(1)
    with scope("barrier"):
        pl.semaphore_wait(barrier, DEVICES - 1)
        row_start(cnt_ref, cnt_ssem, cnt_rsem)
    with scope("fwd2"):
        forward(2)
        forward(3)
    with scope("zt"):
        loads["w2"].wait()
        zt = dot(w2_ref[...], act_ref[...].reshape(HID, TOK), ((0,), (0,)))
        zt = (xt_ref[...].astype(F32) + zt).astype(BF16)

    with scope("cls"):
        loads["heads"].wait()
        loads["lab"].wait()
        cls = lax.broadcasted_iota(jnp.int32, (CLS, TOK), 0)
        for t in range(TASKS):
            head = heads_ref[:, t, :]
            logits = dot(head, zt, ((1,), (0,)))
            ex = jnp.exp(logits - jnp.max(logits, axis=0, keepdims=True))
            prob = ex / jnp.sum(ex, axis=0, keepdims=True)
            onehot = jnp.where(lab_ref[t:t + 1, :] == cls, 1.0, 0.0)
            err = (mask_ref[t:t + 1, :].astype(F32) * (prob - onehot)).astype(BF16)
            dzt = dot(head, err, ((0,), (0,))).astype(BF16)
            dzt_ref[t] = dzt
            dz_ref[:, t * DIM:(t + 1) * DIM] = jnp.transpose(dzt)

    with scope("cntwait"):
        row_all(cnt_ref, cnt_ssem, cnt_rsem).wait_recv()
        total = jnp.sum(cnt_ref[...], axis=0)
        inv = [1.0 / jnp.maximum(lane_pick(total, t), 1.0) for t in range(TASKS)]

    orders = block_orders()

    @scoped
    def compute_b(k):
        part = dot(act_ref[:, k].reshape(512, TOK), dz_ref[...], ((1,), (0,)))
        for t in range(TASKS):
            scaled = (part[:, t * DIM:(t + 1) * DIM] * inv[t]).astype(BF16)
            order = orders[ROUTE[1, k, t][0] - 1]
            for n, j in enumerate(order):
                b1_send[2 * k + t, n // 8, 16 * (n % 8):16 * (n % 8 + 1)] = scaled[16 * j:16 * (j + 1)]

    @scoped
    def compute_a(k, t):
        rows = slice(512 * k, 512 * (k + 1))
        back = dot(w2_ref[rows, :], dzt_ref[t], ((1,), (0,)))
        dpre = (back * slope_ref[rows, :]).astype(BF16)
        part = dot(xsel_ref[ROUTE[0, k, t][0] // 2], dpre, ((1,), (1,)))
        a1_send[2 * k + t] = (part * inv[t]).astype(BF16).reshape(4, 96, 512)

    def s1_bufs(part):
        return ((a1_send, a1_recv), (b1_send, b1_recv))[part]

    def s1_copies(route, n):
        part, k, t = PIECES[route][n]
        send, recv = s1_bufs(part)
        for p, (d, dc) in reversed(list(enumerate(PAIRS))):
            c = flip(core, dc)
            if route == 0:
                g = flip(px, d)
                dev = device(pz, py, g, c)
            elif route == 1:
                g = flip(py, d)
                dev = device(pz, g, px, c)
            else:
                g = flip(zl, d)
                dev = device(2 * zh + g, py, px, c)
            yield remote(send.at[2 * k + t, g * 2 + c], recv.at[2 * k + t, p], ssem.at[part],
                         s1_rsem.at[route, n], dev)

    def s2_copies(route, n):
        part = PIECES[route][n][0]
        if route == 0:
            yield remote(a2_send.at[n, flip(py, 1)], a2_recv.at[n], ssem.at[2], s2_rsem.at[route, n],
                         device(pz, flip(py, 1), px, core))
        elif route == 1:
            yield remote(b2_send.at[n, flip(px, 1)], b2_recv.at[n], ssem.at[3], s2_rsem.at[route, n],
                         device(pz, py, flip(px, 1), core))
        else:
            send, recv = ((ca2_send, ca2_recv), (cb2_send, cb2_recv))[part]
            for p, (dy, dx) in reversed(list(enumerate(PAIRS))):
                y, x = flip(py, dy), flip(px, dx)
                yield remote(send.at[n % 2, 2 * y + x], recv.at[n % 2, p], ssem.at[4 + part],
                             s2_rsem.at[route, n], device(pz, y, x, core))

    def s3_copies(route, n):
        part = PIECES[route][n][0]
        if route == 2:
            send, recv = ((ca3_send, ca3_recv), (cb3_send, cb3_recv))[part]
            yield remote(send.at[n % 2, flip(zh, 1)], recv.at[n % 2], ssem.at[8 + part], s3_rsem.at[route, n],
                         device(lax.rem(pz + 2, 4), py, px, core))
            return
        send, recv = ((a3_send, a3_recv), (b3_send, b3_recv))[part]
        for d in (2, 1, 3):
            z = lax.rem(pz + d, 4)
            yield remote(send.at[n, z], recv.at[n, d - 1], ssem.at[6 + part], s3_rsem.at[route, n],
                         device(z, py, px, core))

    def whole(ref, rsem):
        return remote(ref, ref, rsem, rsem, device(lax.rem(pz + 1, 4), py, px, core))

    @scoped
    def s1_start(route, n):
        for copy in s1_copies(route, n):
            copy.start()

    @scoped
    def s1_finish(route, n):
        part, k, t = PIECES[route][n]
        i = 2 * k + t
        send, recv = s1_bufs(part)
        whole(recv.at[i], s1_rsem.at[route, n]).wait_recv()
        slot = (px, py, zl)[route] * 2 + core
        tot = (send[i, slot].astype(F32) + recv[i, 0].astype(F32)) + (recv[i, 1].astype(F32) + recv[i, 2].astype(F32))
        if route < 2:
            (a2_send, b2_send)[route][n] = tot.reshape(2, PLANE[part] // 2, COLS[part])
        else:
            (ca2_send, cb2_send)[part][n % 2] = tot.reshape(4, PLANE[part] // 4, COLS[part])
        for copy in s2_copies(route, n):
            copy.start()

    @scoped
    def s2_finish(route, n):
        part = PIECES[route][n][0]
        if route < 2:
            send, recv = ((a2_send, a2_recv), (b2_send, b2_recv))[route]
            whole(recv.at[n], s2_rsem.at[route, n]).wait_recv()
            tot = send[n, (py, px)[route]] + recv[n]
            out, count = (a3_send, b3_send)[route].at[n], 4
        else:
            send, recv = ((ca2_send, ca2_recv), (cb2_send, cb2_recv))[part]
            whole(recv.at[n % 2], s2_rsem.at[route, n]).wait_recv()
            tot = (send[n % 2, 2 * py + px] + recv[n % 2, 0]) + (recv[n % 2, 1] + recv[n % 2, 2])
            out, count = (ca3_send, cb3_send)[part].at[n % 2], 2
        if part == 0:
            for z in range(count):
                out[z, 0] = tot[8 * z:8 * (z + 1)]
                shared = 8 * (count + z // 2)
                out[z, 1] = tot[shared:shared + 8]
        else:
            out[...] = tot.reshape(count, 16, DIM)
        for copy in s3_copies(route, n):
            copy.start()

    @scoped
    def s3_finish(route, n):
        part, k, t = PIECES[route][n]
        if route == 2:
            send, recv = ((ca3_send, ca3_recv), (cb3_send, cb3_recv))[part]
            whole(recv.at[n % 2], s3_rsem.at[route, n]).wait_recv()
            tot = send[n % 2, zh] + recv[n % 2]
            odd = zh
        else:
            send, recv = ((a3_send, a3_recv), (b3_send, b3_recv))[part]
            whole(recv.at[n], s3_rsem.at[route, n]).wait_recv()
            tot = (send[n, pz] + recv[n, 0]) + (recv[n, 1] + recv[n, 2])
            odd = zl
        if part == 0:
            low = jnp.where(odd == 0, tot[1, 0:4], tot[1, 4:8])
            for j in range(4):
                gin_ref[t, pl.ds(4 * k + j, 8, stride=12), :] = tot[0, :, 128 * j:128 * (j + 1)]
                gin_ref[t, pl.ds(96 + 4 * k + j, 4, stride=12), :] = low[:, 128 * j:128 * (j + 1)]
        else:
            for j in range(3):
                gout_ref[t, pl.ds(48 * k + j, 16, stride=3), :] = tot[:, 128 * j:128 * (j + 1)]

    compute_b(0)
    s1_start(1, 0)
    s1_start(2, 0)
    loads["sel"].wait()
    for r in range(2):
        xsel_ref[r] = dot(sel_ref[r], xt_ref[...], ((1,), (0,))).astype(BF16)
    compute_a(0, 0)
    s1_start(0, 0)
    compute_a(0, 1)
    s1_start(0, 1)
    compute_b(1)
    s1_start(1, 1)
    s1_start(2, 1)
    compute_a(1, 0)
    compute_a(1, 1)
    for r in (1, 2, 0):
        s1_finish(r, 0)
    s1_start(0, 2)
    s1_start(2, 2)
    compute_b(2)
    s1_start(1, 2)
    compute_a(2, 0)
    for r in (1, 2, 0):
        s1_finish(r, 1)
    s1_start(0, 3)
    s1_start(1, 3)
    for r in (1, 0, 2):
        s2_finish(r, 0)
    compute_a(2, 1)
    s1_start(2, 3)
    for r in (1, 0):
        s1_finish(r, 2)
    for r in (1, 0, 2):
        s2_finish(r, 1)
    for r in (1, 0, 2):
        s3_finish(r, 0)
    for r in (1, 0):
        s1_finish(r, 3)
    s1_finish(2, 2)
    s1_finish(2, 3)
    for r in (1, 0):
        s2_finish(r, 2)
    for r in (1, 0, 2):
        s3_finish(r, 1)
    for r in (1, 0):
        s2_finish(r, 3)
    s2_finish(2, 2)
    s2_finish(2, 3)
    for n in (2, 3):
        for r in (1, 0, 2):
            s3_finish(r, n)

    stores = [pltpu.make_async_copy(src, dst, out_sem.at[i])
              for i, (src, dst) in enumerate(((gin_ref, gin_hbm), (gout_ref, gout_hbm), (gram_out, gram_hbm)))]
    with scope("gram"):
        row = jnp.zeros((1, 128), F32)
        for q, (s, t) in enumerate(((0, 0), (0, 1), (1, 1))):
            prod = gin_ref[s] * gin_ref[t] + gout_ref[s] * gout_ref[t]
            one = jnp.sum(jnp.sum(prod, axis=0, keepdims=True), axis=1, keepdims=True)
            row = jnp.where(lane == q, one, row)
        gram_ref[me] = row
    with scope("gramx"):
        row_start(gram_ref, gram_ssem, gram_rsem)
        stores[0].start()
        stores[1].start()
        for i, ref in enumerate((a1_recv, b1_recv, a2_recv, b2_recv, ca2_recv, cb2_recv, a3_recv, b3_recv,
                                 ca3_recv, cb3_recv)):
            whole(ref, ssem.at[i]).wait_send()
        row_all(cnt_ref, cnt_ssem, cnt_rsem).wait_send()
        stores[0].wait()
        stores[1].wait()
        row_all(gram_ref, gram_ssem, gram_rsem).wait_recv()
    with scope("drain"):
        gram_out[...] = jnp.sum(gram_ref[...], axis=0)
        stores[2].start()
        row_all(gram_ref, gram_ssem, gram_rsem).wait_send()
        stores[2].wait()


def combine(gram_hbm, gin_hbm, gout_hbm, weights_ref, sum_in, sum_out, gram_ref, gin_ref, gout_ref, sem):
    loads = [pltpu.make_async_copy(src, dst, sem.at[i])
             for i, (src, dst) in enumerate(((gram_hbm, gram_ref), (gin_hbm, gin_ref), (gout_hbm, gout_ref)))]
    for load in loads:
        load.start()
    loads[0].wait()
    lane = lax.broadcasted_iota(jnp.int32, (1, 128), 1)
    m00, m01, m11 = [jnp.broadcast_to(jnp.sum(jnp.where(lane == q, gram_ref[...], 0.0), axis=1, keepdims=True), (1, 128))
                     for q in range(3)]
    scale = (m00 + m11) / 2.0
    w0 = jnp.full((1, 128), 0.5, F32)
    w1 = w0
    for _ in range(SOLVER_STEPS):
        r0 = w0 * jnp.exp(-(m00 * w0 + m01 * w1) / scale)
        r1 = w1 * jnp.exp(-(m01 * w0 + m11 * w1) / scale)
        norm = r0 + r1
        w0 = r0 / norm
        w1 = r1 / norm
    weights_ref[0] = w0[0, 0]
    weights_ref[1] = w1[0, 0]
    loads[1].wait()
    loads[2].wait()
    sum_in[...] = w0 * gin_ref[0] + w1 * gin_ref[1]
    sum_out[...] = w0 * gout_ref[0] + w1 * gout_ref[1]


def solution(mesh):
    sel = select_matrices()

    def local_step(x_loc, w_in, w_out, task_heads, lab_loc, mask_loc):
        vmem = pl.BlockSpec(memory_space=pltpu.VMEM)
        hbm = pl.BlockSpec(memory_space=pl.ANY)
        dma = pltpu.SemaphoreType.DMA
        heads_t = jnp.transpose(task_heads, (2, 0, 1))
        args = (x_loc, w_in, w_out, heads_t, lab_loc, mask_loc, jnp.asarray(sel, BF16))
        piece = jax.ShapeDtypeStruct((144, 128), F32)
        outs = [jax.ShapeDtypeStruct((TASKS, 144, 128), F32)] * 2 + [jax.ShapeDtypeStruct((1, 128), F32)]
        scratch = [pltpu.VMEM(a.shape, a.dtype) for a in args] + [pltpu.VMEM(a.shape, a.dtype) for a in outs] + [
            pltpu.VMEM((DIM, TOK), BF16),
            pltpu.VMEM((32, CHUNKS, 16, TOK), BF16),
            pltpu.VMEM((HID, TOK), F32),
            pltpu.VMEM((2, DIM, TOK), BF16),
            pltpu.VMEM((TASKS, DIM, TOK), BF16),
            pltpu.VMEM((TOK, TASKS * DIM), BF16)]
        shapes = [[(BF16, (6, 4), 1), (BF16, (6, 3), 1)], [(F32, (4, 2), 2), (F32, (4,), 2)],
                  [(F32, (4, 4), 0), (F32, (4, 3), 0)], [(F32, (2, 4), 4), (F32, (2, 3), 4)],
                  [(F32, (2, 2), 0), (F32, (2,), 0)]]
        for stage in shapes:
            for dtype, lead, div in stage:
                for part in range(2):
                    rows = (PLANE[part] // div,) if div else TILE[part]
                    scratch.append(pltpu.VMEM(lead + rows + (COLS[part],), dtype))
        scratch += [pltpu.VMEM((DEVICES, 1, 128), F32), pltpu.VMEM((DEVICES, 1, 128), F32),
                    dma((len(args),)), dma((3,)), dma((3, 4)), dma((3, 4)), dma((3, 4)), dma((10,)),
                    dma, dma, dma, dma]
        gin, gout, gram = pl.pallas_call(
            kernel,
            out_shape=outs,
            in_specs=[hbm] * len(args),
            out_specs=[hbm] * 3,
            scratch_shapes=scratch,
            compiler_params=pltpu.CompilerParams(collective_id=0, has_side_effects=True,
                                                 vmem_limit_bytes=66_900_000),
            name="step",
        )(*args)
        weights, grad_in, grad_out = pl.pallas_call(
            combine,
            out_shape=[jax.ShapeDtypeStruct((TASKS,), F32), piece, piece],
            in_specs=[hbm] * 3,
            out_specs=[pl.BlockSpec(memory_space=pltpu.SMEM), vmem, vmem],
            scratch_shapes=[pltpu.VMEM(outs[2].shape, F32), pltpu.VMEM(outs[0].shape, F32),
                            pltpu.VMEM(outs[1].shape, F32), dma((3,))],
            compiler_params=pltpu.CompilerParams(vmem_limit_bytes=66_900_000),
            name="combine",
        )(gram, gin, gout)
        return weights, grad_in.reshape(-1), grad_out.reshape(-1)

    return jax.shard_map(local_step, mesh=mesh,
                         in_specs=(P("data", None), P(), P(), P(), P(None, "data"), P(None, "data")),
                         out_specs=(P(), P("data"), P("data")), check_vma=False)
```

time: 304 us -> 66.7 us (0.22)
  waiting for transfers between devices: 99.5 us -> 0 us
  blocking collectives: 79.7 us -> 0 us
  Pallas kernels: 0 us -> 65.9 us
  other arithmetic: 42.6 us -> 0 us
  matrix products: 36 us -> 0 us
  local copies, waits for them, and re-layouts: 33.9 us -> 0 us
  starting transfers between devices: 8.4 us -> 0 us
    all_to_all x2 -> x0, waiting for transfers between devices: 99.5 us -> none  [local_step(): arrived = lax.all_to_all(scaled, 'data', 1, 1, tiled=True)]
    psum x2 -> x0, blocking collectives: 79.7 us -> none  [the longest x1 41.9 us: local_step(): label_count = lax.psum(mask_loc.sum(axis=1), 'data')]
    pallas_call x0 -> x2, Pallas kernels: none -> 65.9 us  [the longest x1 64 us: local_step(): pl.pallas_call(kernel, out_shape=outs, in_specs=[hbm] * len(args), out_sp...]
    dot_general x7 -> x0, matrix products: 36 us -> none  [the longest x1 12.3 us: device_grads(): jnp.einsum('bd,tbf->tdf', x_loc, d_pre, preferred_element_type=jnp.float32)]
    reduce_sum x45 -> x0, other arithmetic: 23.7 us -> none  [the longest x20 12.4 us: solver_step(): return raised / raised.sum()]
    div x21 -> x0, other arithmetic: 13 us -> none  [the longest x20 13 us: solver_step(): return raised / raised.sum()]
    transpose x2 -> x0, local copies, waits for them, and re-layouts: 12.1 us -> none  [the longest x1 6.06 us: device_grads(): jnp.einsum('bd,tbf->tdf', x_loc, d_pre, preferred_element_type=jnp.float32)]
    reshape x2 -> x0, local copies, waits for them, and re-layouts: 11.4 us -> none  [local_step(): grad_full.reshape(num_tasks, group_size, -1) * inv_count[:, None, None]]
  transfers between devices with their start and end apart: 2 -> 0, of which waited for: 2 -> 0; matrix products, arithmetic and copies ran while one was open for 3% -> 0% of each run, Pallas kernels for 0% -> 0%
where the time goes in v2:
time: 66.7 us; the launch traced here: 66.5 us
  Pallas kernels  65.9 us (99%)
    pallas_call x1, Pallas kernels, local_step(): pl.pallas_call(kernel, out_shape=outs, in_specs=[hbm] * len(args), out_sp...  64 us
    pallas_call x1, Pallas kernels, local_step(): pl.pallas_call(combine, out_shape=[jax.ShapeDtypeStruct((TASKS,), F32), p...  1.91 us

profile of v2, /device:TPU:0, one launch (start us, length us, event | category | flops | bytes accessed | tf_op | source)
XLA Modules:
  0.0 66.5 jit_solution(6229118041544438699)
XLA Ops:
  0.6 64.0 %step.1 = (f32[2,144,128]{2,1,0:T(8,128)}, f32[2,144,128]{2,1,0:T(8,128)}, f32[1,128]{1,0:T(1,128)}) custom-call(bf16[1024,384]{1,0:T(8,128)(2,1)} %x_hbm.1, bf16[384,1536]{1,0:T(8,128)(2,1)} %w1_hbm.1, bf16[1536,384]{1,0:T(8,128)(2,1)} %w2_hbm.1, bf16[10,2,384]{2,1,0:T(2,128)(2,1)} %bitcast.3, s32[2,1024]{1,0:T(2,128)} %lab_hbm.1, s32[2,1024]{1,0:T(2,128)} %mask_hbm.1, ...), custom_call_target="tpu_custom_call" | custom-call | tf_op jit(solution)/shard_map/step/pallas_call | solution.py:457
  64.6 1.9 %combine.1 = (f32[2]{0:T(128)}, f32[144,128]{1,0:T(8,128)}, f32[144,128]{1,0:T(8,128)}) custom-call(f32[1,128]{1,0:T(1,128)} %get-tuple-element.9.gram_hbm, f32[2,144,128]{2,1,0:T(8,128)} %get-tuple-element.10.gin_hbm, f32[2,144,128]{2,1,0:T(8,128)} %get-tuple-element.11.gout_hbm), custom_call_target="tpu_custom_call" | custom-call | tf_op jit(solution)/shard_map/combine/pallas_call | solution.py:467

commit v3 on v2

v3 whole, which is shorter than its diff:
```python
import contextlib
import math

import jax
import jax.numpy as jnp
import numpy as np
from jax import lax
from jax.experimental import pallas as pl
from jax.experimental.pallas import tpu as pltpu
from jax.sharding import PartitionSpec as P

SOLVER_STEPS = 20
DEVICES = 32
DIM, HID, TOK, CLS = 384, 1536, 1024, 10
CHUNKS, TASKS = 3, 2
F32, BF16 = jnp.float32, jnp.bfloat16
GELU_C = 0.7978845608028654
GELU_A = 0.044715
PAIRS = ((0, 1), (1, 0), (1, 1))

PIECES = (((1, 0, 1), (0, 0, 1), (0, 1, 0), (0, 2, 0)),
          ((1, 0, 0), (1, 1, 0), (1, 2, 0), (1, 2, 1)),
          ((0, 0, 0), (1, 1, 1), (0, 1, 1), (0, 2, 1)))
ROUTE = {piece: (r, n) for r, pieces in enumerate(PIECES) for n, piece in enumerate(pieces)}
COLS = (512, DIM)
PLANE = (96, 128)
TILE = ((3, 8, 256), (16, DIM))


def no_scope(name):
    return contextlib.nullcontext()


scope = no_scope


def owner(z, y, x, c):
    return 8 * z + 4 * y + 2 * x + c


def tiles(owners):
    return [12 * o + i for o in owners for i in range(8)] + [12 * o + i for o in owners for i in range(8, 12)]


def owners(route):
    two = range(2)
    if route == 0:
        return [[[owner(z, y, x, c) for z in range(4)] for y in two] for x in two for c in two]
    if route == 1:
        return [[[owner(z, y, x, c) for z in range(4)] for x in two] for y in two for c in two]
    return [[[owner(2 * zh + zl, y, x, c) for zh in two] for y in two for x in two] for zl in two for c in two]


def select_matrices():
    mat = np.zeros((2, DIM, DIM), np.float32)
    for m, route in zip(mat, (0, 2)):
        order = [r for first in owners(route) for second in first for r in tiles(second)]
        m[np.arange(DIM), np.array(order)] = 1.0
    return mat


def scoped(f):
    def call(*args):
        with scope("_".join([f.__name__, *map(str, args)])):
            return f(*args)
    return call


def dot(a, b, dims):
    return lax.dot_general(a, b, (dims, ((), ())), preferred_element_type=F32)


def kernel(x_hbm, w1_hbm, w2_hbm, heads_hbm, lab_hbm, mask_hbm, sel_hbm,
           gin_hbm, gout_hbm, gram_hbm,
           x_ref, w1_ref, w2_ref, heads_ref, lab_ref, mask_ref, sel_ref,
           gin_ref, gout_ref, gram_out,
           xt_ref, act_ref, pre_ref, cdf_ref, xsel_ref, dzt_ref, dz_ref, cnt_ref, gram_ref, *rest):
    bufs = {piece: rest[6 * i:6 * (i + 1)] for i, piece in enumerate(ROUTE)}
    in_sem, out_sem, s1_rsem, s2_rsem, s3_rsem, ssem, cnt_ssem, cnt_rsem, gram_ssem, gram_rsem = rest[6 * len(bufs):]
    me = lax.axis_index("data")
    core = lax.rem(me, 2)
    px = lax.rem(me // 2, 2)
    py = lax.rem(me // 4, 2)
    pz = me // 8
    zl, zh = lax.rem(pz, 2), pz // 2

    def device(z, y, x, c):
        return (owner(z, y, x, c),)

    def flip(v, d):
        return lax.rem(v + d, 2)

    def remote(src, dst, ssem, rsem, dev):
        return pltpu.make_async_remote_copy(src_ref=src, dst_ref=dst, send_sem=ssem, recv_sem=rsem,
                                            device_id=dev, device_id_type=pl.DeviceIdType.MESH)

    loads = {name: pltpu.make_async_copy(src, dst, in_sem.at[i]) for i, (name, src, dst) in enumerate((
        ("mask", mask_hbm, mask_ref), ("x", x_hbm, x_ref), ("w1", w1_hbm, w1_ref), ("w2", w2_hbm, w2_ref),
        ("heads", heads_hbm, heads_ref), ("lab", lab_hbm, lab_ref), ("sel", sel_hbm, sel_ref)))}
    for load in loads.values():
        load.start()

    barrier = pltpu.get_barrier_semaphore()

    @pl.loop(1, DEVICES)
    def _(d):
        pl.semaphore_signal(barrier, inc=1, device_id=(lax.rem(me + d, DEVICES),),
                            device_id_type=pl.DeviceIdType.MESH)

    def row_copy(buf, ssem, rsem, d):
        return remote(buf.at[me], buf.at[me], ssem, rsem, (lax.rem(me + d, DEVICES),))

    def row_start(buf, ssem, rsem):
        @pl.loop(1, DEVICES)
        def _(d):
            row_copy(buf, ssem, rsem, d).start()

    def row_all(buf, ssem, rsem):
        rows = buf.at[pl.ds(0, DEVICES - 1)]
        return remote(rows, rows, ssem, rsem, (lax.rem(me + 1, DEVICES),))

    lane = lax.broadcasted_iota(jnp.int32, (1, 128), 1)

    def lane_pick(row, k):
        return jnp.sum(jnp.where(lane == k, row, 0.0), axis=1, keepdims=True)

    loads["mask"].wait()
    counts = jnp.sum(mask_ref[...].astype(F32), axis=1, keepdims=True)
    cnt_ref[me] = jnp.where(lane == 0, counts[0:1], jnp.where(lane == 1, counts[1:2], 0.0))

    def forward(i):
        cols = slice(i * 384, (i + 1) * 384)
        pre = dot(w1_ref[:, cols], xt_ref[...], ((0,), (0,)))
        cdf = 0.5 + 0.5 * jnp.tanh(pre * (GELU_C + (GELU_C * GELU_A) * (pre * pre)))
        act_ref[8 * i:8 * (i + 1)] = (pre * cdf).astype(BF16).reshape(8, CHUNKS, 16, TOK)
        pre_ref[cols, :] = pre
        cdf_ref[cols, :] = cdf

    with scope("xt"):
        loads["x"].wait()
        xt_ref[...] = jnp.transpose(x_ref[...])
    with scope("fwd"):
        loads["w1"].wait()
        forward(0)
        forward(1)
    with scope("barrier"):
        pl.semaphore_wait(barrier, DEVICES - 1)
        row_start(cnt_ref, cnt_ssem, cnt_rsem)
    with scope("fwd2"):
        forward(2)
        forward(3)
    with scope("zt"):
        loads["w2"].wait()
        zt = dot(w2_ref[...], act_ref[...].reshape(HID, TOK), ((0,), (0,)))
        zt = (xt_ref[...].astype(F32) + zt).astype(BF16)

    with scope("cls"):
        loads["heads"].wait()
        loads["lab"].wait()
        cls = lax.broadcasted_iota(jnp.int32, (CLS, TOK), 0)
        for t in range(TASKS):
            head = heads_ref[:, t, :]
            logits = dot(head, zt, ((1,), (0,)))
            ex = jnp.exp(logits - jnp.max(logits, axis=0, keepdims=True))
            prob = ex / jnp.sum(ex, axis=0, keepdims=True)
            onehot = jnp.where(lab_ref[t:t + 1, :] == cls, 1.0, 0.0)
            err = (mask_ref[t:t + 1, :].astype(F32) * (prob - onehot)).astype(BF16)
            dzt = dot(head, err, ((0,), (0,))).astype(BF16)
            dzt_ref[t] = dzt
            dz_ref[:, t * DIM:(t + 1) * DIM] = jnp.transpose(dzt)

    inv = []

    def wait_counts():
        with scope("cntwait"):
            row_all(cnt_ref, cnt_ssem, cnt_rsem).wait_recv()
            total = jnp.sum(cnt_ref[...], axis=0)
            inv.extend(1.0 / jnp.maximum(lane_pick(total, t), 1.0) for t in range(TASKS))

    @scoped
    def compute_b(k, *tasks):
        part = dot(act_ref[:, k].reshape(512, TOK), dz_ref[:, tasks[0] * DIM:(tasks[-1] + 1) * DIM], ((1,), (0,)))
        if not inv:
            wait_counts()
        for i, t in enumerate(tasks):
            scaled = (part[:, i * DIM:(i + 1) * DIM] * inv[t]).astype(BF16)
            send = bufs[1, k, t][0]
            for slot, first in enumerate(owners(ROUTE[1, k, t][0])):
                for n, j in enumerate(o for second in first for o in second):
                    send[slot, 16 * n:16 * (n + 1)] = scaled[16 * j:16 * (j + 1)]

    @scoped
    def compute_a(k, t):
        rows = slice(512 * k, 512 * (k + 1))
        back = dot(w2_ref[rows, :], dzt_ref[t], ((1,), (0,)))
        pre, cdf = pre_ref[rows, :], cdf_ref[rows, :]
        slope = cdf + (pre * cdf) * (1.0 - cdf) * (2.0 * GELU_C + (6.0 * GELU_C * GELU_A) * (pre * pre))
        dpre = (back * slope).astype(BF16)
        part = dot(xsel_ref[ROUTE[0, k, t][0] // 2], dpre, ((1,), (1,)))
        bufs[0, k, t][0][...] = (part * inv[t]).astype(BF16).reshape(4, 96, 512)

    def select_rows(r):
        xsel_ref[r] = dot(sel_ref[r], xt_ref[...], ((1,), (0,))).astype(BF16)

    def s1_copies(route, n):
        send, recv = bufs[PIECES[route][n]][:2]
        for p, (d, dc) in reversed(list(enumerate(PAIRS))):
            c = flip(core, dc)
            g = flip((px, py, zl)[route], d)
            dev = (device(pz, py, g, c), device(pz, g, px, c), device(2 * zh + g, py, px, c))[route]
            yield remote(send.at[g * 2 + c], recv.at[p], ssem.at[0], s1_rsem.at[route, n], dev)

    def s2_copies(route, n):
        send, recv = bufs[PIECES[route][n]][2:4]
        if route == 2:
            for p, (dy, dx) in reversed(list(enumerate(PAIRS))):
                y, x = flip(py, dy), flip(px, dx)
                yield remote(send.at[2 * y + x], recv.at[p], ssem.at[1], s2_rsem.at[route, n],
                             device(pz, y, x, core))
            return
        g = flip((py, px)[route], 1)
        dev = (device(pz, g, px, core), device(pz, py, g, core))[route]
        yield remote(send.at[g], recv.at[0], ssem.at[1], s2_rsem.at[route, n], dev)

    def s3_copies(route, n):
        send, recv = bufs[PIECES[route][n]][4:6]
        if route == 2:
            yield remote(send.at[flip(zh, 1)], recv.at[0], ssem.at[2], s3_rsem.at[route, n],
                         device(lax.rem(pz + 2, 4), py, px, core))
            return
        for d in (2, 1, 3):
            z = lax.rem(pz + d, 4)
            yield remote(send.at[z], recv.at[d - 1], ssem.at[2], s3_rsem.at[route, n], device(z, py, px, core))

    def whole(ref, sem):
        return remote(ref, ref, sem, sem, device(lax.rem(pz + 1, 4), py, px, core))

    def total_of(own, recv, sem):
        whole(recv, sem).wait_recv()
        terms = [own.astype(F32)] + [recv[i].astype(F32) for i in range(recv.shape[0])]
        while len(terms) > 1:
            terms = [a + b for a, b in zip(terms[::2], terms[1::2])]
        return terms[0]

    @scoped
    def s1_start(route, n):
        for copy in s1_copies(route, n):
            copy.start()

    @scoped
    def s1_finish(route, n):
        send, recv, out = bufs[PIECES[route][n]][:3]
        tot = total_of(send[(px, py, zl)[route] * 2 + core], recv, s1_rsem.at[route, n])
        out[...] = tot.reshape(out.shape)
        for copy in s2_copies(route, n):
            copy.start()

    @scoped
    def s2_finish(route, n):
        part = PIECES[route][n][0]
        send, recv, out = bufs[PIECES[route][n]][2:5]
        tot = total_of(send[(py, px, 2 * py + px)[route]], recv, s2_rsem.at[route, n])
        count = out.shape[0]
        if part == 0:
            for z in range(count):
                top = tot[8 * z:8 * (z + 1)]
                low = tot[8 * count + 4 * z:8 * count + 4 * (z + 1)]
                out[z, 0] = top[:, :256]
                out[z, 1] = top[:, 256:]
                out[z, 2] = jnp.concatenate([low[:, :256], low[:, 256:]], axis=0)
        else:
            out[...] = tot.reshape(out.shape)
        for copy in s3_copies(route, n):
            copy.start()

    @scoped
    def s3_finish(route, n):
        part, k, t = PIECES[route][n]
        send, recv = bufs[PIECES[route][n]][4:6]
        tot = total_of(send[zh if route == 2 else pz], recv, s3_rsem.at[route, n])
        if part == 0:
            for j in range(4):
                cols = slice(128 * (j % 2), 128 * (j % 2 + 1))
                gin_ref[t, pl.ds(4 * k + j, 8, stride=12), :] = tot[j // 2, :, cols]
                gin_ref[t, pl.ds(96 + 4 * k + j, 4, stride=12), :] = tot[2, 4 * (j // 2):4 * (j // 2 + 1), cols]
        else:
            for j in range(3):
                gout_ref[t, pl.ds(48 * k + j, 16, stride=3), :] = tot[:, 128 * j:128 * (j + 1)]

    x, y, z = range(3)

    def each(f, n, *routes):
        for r in routes:
            f(r, n)

    compute_b(0, 0)
    s1_start(y, 0)
    compute_b(0, 1)
    s1_start(x, 0)
    loads["sel"].wait()
    select_rows(1)
    compute_a(0, 0)
    s1_start(z, 0)
    select_rows(0)
    compute_a(0, 1)
    s1_start(x, 1)
    compute_b(1, 0, 1)
    each(s1_start, 1, y, z)
    compute_a(1, 0)
    each(s1_finish, 0, y, x)
    s1_start(x, 2)
    compute_b(2, 0, 1)
    s1_start(y, 2)
    compute_a(1, 1)
    s1_start(z, 2)
    each(s1_finish, 1, y, x)
    s1_start(y, 3)
    compute_a(2, 0)
    s1_start(x, 3)
    compute_a(2, 1)
    s1_start(z, 3)
    each(s2_finish, 0, y, x)
    each(s1_finish, 2, y, x)
    each(s2_finish, 1, y, x)
    each(s1_finish, 3, y, x)
    for n in range(4):
        s1_finish(z, n)
    for n in (2, 3):
        each(s3_finish, n - 2, y, x)
        each(s2_finish, n, y, x)
    for n in range(4):
        s2_finish(z, n)
    for n in (2, 3):
        each(s3_finish, n, y, x)
    for n in range(4):
        s3_finish(z, n)

    stores = [pltpu.make_async_copy(src, dst, out_sem.at[i])
              for i, (src, dst) in enumerate(((gin_ref, gin_hbm), (gout_ref, gout_hbm), (gram_out, gram_hbm)))]
    with scope("gram"):
        row = jnp.zeros((1, 128), F32)
        for q, (s, t) in enumerate(((0, 0), (0, 1), (1, 1))):
            prod = gin_ref[s] * gin_ref[t] + gout_ref[s] * gout_ref[t]
            one = jnp.sum(jnp.sum(prod, axis=0, keepdims=True), axis=1, keepdims=True)
            row = jnp.where(lane == q, one, row)
        gram_ref[me] = row
    with scope("gramx"):
        row_start(gram_ref, gram_ssem, gram_rsem)
        stores[0].start()
        stores[1].start()
        for stage in range(3):
            sent = sum(math.prod(b[2 * stage + 1].shape) * (2 if stage == 0 else 4) for b in bufs.values())
            whole(pre_ref.at[pl.ds(0, sent // (4 * TOK))], ssem.at[stage]).wait_send()
        row_all(cnt_ref, cnt_ssem, cnt_rsem).wait_send()
        stores[0].wait()
        stores[1].wait()
        row_all(gram_ref, gram_ssem, gram_rsem).wait_recv()
    with scope("drain"):
        gram_out[...] = jnp.sum(gram_ref[...], axis=0)
        stores[2].start()
        row_all(gram_ref, gram_ssem, gram_rsem).wait_send()
        stores[2].wait()


def combine(gram_hbm, gin_hbm, gout_hbm, weights_ref, sum_in, sum_out, gram_ref, gin_ref, gout_ref, sem):
    loads = [pltpu.make_async_copy(src, dst, sem.at[i])
             for i, (src, dst) in enumerate(((gram_hbm, gram_ref), (gin_hbm, gin_ref), (gout_hbm, gout_ref)))]
    for load in loads:
        load.start()
    loads[0].wait()
    lane = lax.broadcasted_iota(jnp.int32, (1, 128), 1)
    m00, m01, m11 = [jnp.broadcast_to(jnp.sum(jnp.where(lane == q, gram_ref[...], 0.0), axis=1, keepdims=True), (1, 128))
                     for q in range(3)]
    scale = (m00 + m11) / 2.0
    w0 = jnp.full((1, 128), 0.5, F32)
    w1 = w0
    for _ in range(SOLVER_STEPS):
        r0 = w0 * jnp.exp(-(m00 * w0 + m01 * w1) / scale)
        r1 = w1 * jnp.exp(-(m01 * w0 + m11 * w1) / scale)
        norm = r0 + r1
        w0 = r0 / norm
        w1 = r1 / norm
    weights_ref[0] = w0[0, 0]
    weights_ref[1] = w1[0, 0]
    loads[1].wait()
    loads[2].wait()
    sum_in[...] = w0 * gin_ref[0] + w1 * gin_ref[1]
    sum_out[...] = w0 * gout_ref[0] + w1 * gout_ref[1]


def solution(mesh):
    sel = select_matrices()

    def local_step(x_loc, w_in, w_out, task_heads, lab_loc, mask_loc):
        vmem = pl.BlockSpec(memory_space=pltpu.VMEM)
        hbm = pl.BlockSpec(memory_space=pl.ANY)
        dma = pltpu.SemaphoreType.DMA
        heads_t = jnp.transpose(task_heads, (2, 0, 1))
        args = (x_loc, w_in, w_out, heads_t, lab_loc, mask_loc, jnp.asarray(sel, BF16))
        piece = jax.ShapeDtypeStruct((144, 128), F32)
        outs = [jax.ShapeDtypeStruct((TASKS, 144, 128), F32)] * 2 + [jax.ShapeDtypeStruct((1, 128), F32)]
        scratch = [pltpu.VMEM(a.shape, a.dtype) for a in args] + [pltpu.VMEM(a.shape, a.dtype) for a in outs] + [
            pltpu.VMEM((DIM, TOK), BF16),
            pltpu.VMEM((32, CHUNKS, 16, TOK), BF16),
            pltpu.VMEM((HID, TOK), F32),
            pltpu.VMEM((HID, TOK), F32),
            pltpu.VMEM((2, DIM, TOK), BF16),
            pltpu.VMEM((TASKS, DIM, TOK), BF16),
            pltpu.VMEM((TOK, TASKS * DIM), BF16),
            pltpu.VMEM((DEVICES, 1, 128), F32),
            pltpu.VMEM((DEVICES, 1, 128), F32)]
        for (part, k, t), (route, n) in ROUTE.items():
            fan = 4 if route == 2 else 2
            rows, cols = PLANE[part], COLS[part]
            scratch += [pltpu.VMEM((4, rows, cols), BF16), pltpu.VMEM((3, rows, cols), BF16),
                        pltpu.VMEM((fan, rows // fan, cols), F32), pltpu.VMEM((fan - 1, rows // fan, cols), F32),
                        pltpu.VMEM((8 // fan,) + TILE[part], F32), pltpu.VMEM((8 // fan - 1,) + TILE[part], F32)]
        scratch += [dma((len(args),)), dma((3,)), dma((3, 4)), dma((3, 4)), dma((3, 4)), dma((3,)),
                    dma, dma, dma, dma]
        gin, gout, gram = pl.pallas_call(
            kernel,
            out_shape=outs,
            in_specs=[hbm] * len(args),
            out_specs=[hbm] * 3,
            scratch_shapes=scratch,
            compiler_params=pltpu.CompilerParams(collective_id=0, has_side_effects=True,
                                                 vmem_limit_bytes=66_900_000),
            name="step",
        )(*args)
        weights, grad_in, grad_out = pl.pallas_call(
            combine,
            out_shape=[jax.ShapeDtypeStruct((TASKS,), F32), piece, piece],
            in_specs=[hbm] * 3,
            out_specs=[pl.BlockSpec(memory_space=pltpu.SMEM), vmem, vmem],
            scratch_shapes=[pltpu.VMEM(outs[2].shape, F32), pltpu.VMEM(outs[0].shape, F32),
                            pltpu.VMEM(outs[1].shape, F32), dma((3,))],
            compiler_params=pltpu.CompilerParams(vmem_limit_bytes=66_900_000),
            name="combine",
        )(gram, gin, gout)
        return weights, grad_in.reshape(-1), grad_out.reshape(-1)

    return jax.shard_map(local_step, mesh=mesh,
                         in_specs=(P("data", None), P(), P(), P(), P(None, "data"), P(None, "data")),
                         out_specs=(P(), P("data"), P("data")), check_vma=False)
```

time: 66.7 us -> 60.8 us (0.912)
  Pallas kernels: 65.9 us -> 60 us
    pallas_call x1, Pallas kernels: 64 us -> 58.1 us  [local_step(): pl.pallas_call(kernel, out_shape=outs, in_specs=[hbm] * len(args), out_sp...]
where the time goes in v3:
time: 60.8 us; the launch traced here: 60.6 us
  Pallas kernels  60 us (99%)
  between operations  0.64 us (1%)
    pallas_call x1, Pallas kernels, local_step(): pl.pallas_call(kernel, out_shape=outs, in_specs=[hbm] * len(args), out_sp...  58.1 us
    pallas_call x1, Pallas kernels, local_step(): pl.pallas_call(combine, out_shape=[jax.ShapeDtypeStruct((TASKS,), F32), p...  1.91 us

profile of v3, /device:TPU:0, one launch (start us, length us, event | category | flops | bytes accessed | tf_op | source)
XLA Modules:
  0.0 60.6 jit_solution(4429884745129840533)
XLA Ops:
  0.6 58.1 %step.1 = (f32[2,144,128]{2,1,0:T(8,128)}, f32[2,144,128]{2,1,0:T(8,128)}, f32[1,128]{1,0:T(1,128)}) custom-call(bf16[1024,384]{1,0:T(8,128)(2,1)} %x_hbm.1, bf16[384,1536]{1,0:T(8,128)(2,1)} %w1_hbm.1, bf16[1536,384]{1,0:T(8,128)(2,1)} %w2_hbm.1, bf16[10,2,384]{2,1,0:T(2,128)(2,1)} %bitcast.3, s32[2,1024]{1,0:T(2,128)} %lab_hbm.1, s32[2,1024]{1,0:T(2,128)} %mask_hbm.1, ...), custom_call_target="tpu_custom_call" | custom-call | tf_op jit(solution)/shard_map/step/pallas_call | solution.py:420
  58.7 1.9 %combine.1 = (f32[2]{0:T(128)}, f32[144,128]{1,0:T(8,128)}, f32[144,128]{1,0:T(8,128)}) custom-call(f32[1,128]{1,0:T(1,128)} %get-tuple-element.9.gram_hbm, f32[2,144,128]{2,1,0:T(8,128)} %get-tuple-element.10.gin_hbm, f32[2,144,128]{2,1,0:T(8,128)} %get-tuple-element.11.gout_hbm), custom_call_target="tpu_custom_call" | custom-call | tf_op jit(solution)/shard_map/combine/pallas_call | solution.py:430

commit v4 on v3

v4 whole, which is shorter than its diff:
```python
import contextlib
import itertools
import math

import jax
import jax.numpy as jnp
import numpy as np
from jax import lax
from jax.experimental import pallas as pl
from jax.experimental.pallas import tpu as pltpu
from jax.sharding import PartitionSpec as P

SOLVER_STEPS = 20
DEVICES = 32
DIM, HID, TOK, CLS = 384, 1536, 1024, 10
CHUNKS, TASKS = 3, 2
F32, BF16 = jnp.float32, jnp.bfloat16
GELU_C = 0.7978845608028654
GELU_A = 0.044715

ROUTES = {"x": ("x", "y", "zl", "zh"), "y": ("y", "x", "zl", "zh"), "z": ("zl", "xy", "zh"),
          "zyx": ("zl", "y", "x", "zh"), "zxy": ("zl", "x", "y", "zh")}
X = ((1, 0, 1), (0, 0, 1), (0, 1, 0), (0, 2, 0))
Y = ((1, 0, 0), (1, 1, 0), (1, 2, 0), (1, 2, 1))
Z = ((0, 0, 0), (1, 1, 1), (0, 1, 1), (0, 2, 1))
PATH = dict.fromkeys(X, ROUTES["x"]) | dict.fromkeys(Y, ROUTES["y"]) | {
    Z[0]: ROUTES["zyx"], Z[1]: ROUTES["zxy"], Z[2]: ROUTES["z"], Z[3]: ROUTES["z"]}
NUMBER = {piece: i for i, piece in enumerate(PATH)}
COLS = (512, DIM)
PLANE = (96, 128)
TILE = ((3, 8, 256), (16, DIM))


def no_scope(name):
    return contextlib.nullcontext()


scope = no_scope


def owner(z, y, x, c):
    return 8 * z + 4 * y + 2 * x + c


def tiles(owners):
    return [12 * o + i for o in owners for i in range(8)] + [12 * o + i for o in owners for i in range(8, 12)]


def axes_of(stage):
    return ("y", "x") if stage == "xy" else (stage,)


def owners(path):
    def points(axes):
        return [dict(zip(axes, bits)) for bits in itertools.product(range(2), repeat=len(axes))]

    def number(at):
        return owner(2 * at["zh"] + at["zl"], at["y"], at["x"], at["c"])

    rest = [axis for stage in path[2:] for axis in axes_of(stage)]
    return [[[number(p | q | r) for r in points(rest)] for q in points(axes_of(path[1]))] for p in points((path[0], "c"))]


def orders_of_rows():
    paths = list(dict.fromkeys(path for piece, path in PATH.items() if piece[0] == 0))
    orders = [tuple(r for first in owners(path) for second in first for r in tiles(second)) for path in paths]
    kinds = list(dict.fromkeys(orders))
    return kinds, {path: kinds.index(order) for path, order in zip(paths, orders)}


ORDERS, ORDER_OF = orders_of_rows()


def select_matrices():
    mat = np.zeros((len(ORDERS), DIM, DIM), np.float32)
    for m, order in zip(mat, ORDERS):
        m[np.arange(DIM), np.array(order)] = 1.0
    return mat


def buffers(part, path):
    rows, cols, fan = PLANE[part], COLS[part], 2 ** len(axes_of(path[1]))
    shapes = [((4, rows, cols), BF16), ((3, rows, cols), BF16),
              ((fan, rows // fan, cols), F32), ((fan - 1, rows // fan, cols), F32)]
    for left in range(len(path) - 3, -1, -1):
        shapes += [((2,) * (left + 1) + TILE[part], F32), ((1,) + (2,) * left + TILE[part], F32)]
    return shapes


def scoped(f):
    def call(*args):
        with scope("_".join([f.__name__, *map(str, args)])):
            return f(*args)
    return call


def dot(a, b, dims):
    return lax.dot_general(a, b, (dims, ((), ())), preferred_element_type=F32)


def kernel(x_hbm, w1_hbm, w2_hbm, heads_hbm, lab_hbm, mask_hbm, sel_hbm,
           gin_hbm, gout_hbm, gram_out,
           x_ref, w1_ref, w2_ref, heads_ref, lab_ref, mask_ref, sel_ref,
           gin_ref, gout_ref, xt_ref, act_ref, pre_ref, cdf_ref, xsel_ref, dzt_ref, dz_ref, cnt_ref, gram_ref, *rest):
    rest = list(rest)
    bufs = {piece: [rest.pop(0) for _ in range(2 * len(path))] for piece, path in PATH.items()}
    in_sem, out_sem, rsem, ssem, cnt_ssem, cnt_rsem, gram_ssem, gram_rsem = rest
    me = lax.axis_index("data")
    core = lax.rem(me, 2)
    px = lax.rem(me // 2, 2)
    py = lax.rem(me // 4, 2)
    pz = me // 8
    zl, zh = lax.rem(pz, 2), pz // 2

    here = {"x": px, "y": py, "c": core, "zl": zl, "zh": zh}

    def peer(at):
        at = here | at
        return (owner(2 * at["zh"] + at["zl"], at["y"], at["x"], at["c"]),)

    def flip(v, d):
        return lax.rem(v + d, 2)

    def remote(src, dst, ssem, rsem, dev):
        return pltpu.make_async_remote_copy(src_ref=src, dst_ref=dst, send_sem=ssem, recv_sem=rsem,
                                            device_id=dev, device_id_type=pl.DeviceIdType.MESH)

    loads = {name: pltpu.make_async_copy(src, dst, in_sem.at[i]) for i, (name, src, dst) in enumerate((
        ("x", x_hbm, x_ref), ("w1", w1_hbm, w1_ref), ("mask", mask_hbm, mask_ref), ("w2", w2_hbm, w2_ref),
        ("heads", heads_hbm, heads_ref), ("lab", lab_hbm, lab_ref), ("sel", sel_hbm, sel_ref)))}
    for load in loads.values():
        load.start()

    others = []
    for z in (3 - pz, lax.rem(pz + 2, 4), pz + 1 - 2 * zl, pz):
        for dy, dx, dc in itertools.product((1, 0), repeat=3):
            others.append((owner(z, flip(py, dy), flip(px, dx), flip(core, dc)),))
    others.pop()

    barrier = pltpu.get_barrier_semaphore()
    for dev in others:
        pl.semaphore_signal(barrier, inc=1, device_id=dev, device_id_type=pl.DeviceIdType.MESH)

    def row_start(buf, ssem, rsem):
        for dev in others:
            remote(buf.at[me], buf.at[me], ssem, rsem, dev).start()

    def row_all(buf, ssem, rsem):
        rows = buf.at[pl.ds(0, DEVICES - 1)]
        return remote(rows, rows, ssem, rsem, others[0])

    lane = lax.broadcasted_iota(jnp.int32, (1, 128), 1)

    def lane_pick(row, k):
        return jnp.sum(jnp.where(lane == k, row, 0.0), axis=1, keepdims=True)

    def forward(i):
        cols = slice(i * 384, (i + 1) * 384)
        pre = dot(w1_ref[:, cols], xt_ref[...], ((0,), (0,)))
        cdf = 0.5 + 0.5 * jnp.tanh(pre * (GELU_C + (GELU_C * GELU_A) * (pre * pre)))
        act_ref[8 * i:8 * (i + 1)] = (pre * cdf).astype(BF16).reshape(8, CHUNKS, 16, TOK)
        pre_ref[cols, :] = pre
        cdf_ref[cols, :] = cdf

    with scope("xt"):
        loads["x"].wait()
        xt_ref[...] = jnp.transpose(x_ref[...])
    with scope("fwd"):
        loads["w1"].wait()
        forward(0)
        forward(1)
        loads["mask"].wait()
        counts = jnp.sum(mask_ref[...].astype(F32), axis=1, keepdims=True)
        cnt_ref[me] = jnp.where(lane == 0, counts[0:1], jnp.where(lane == 1, counts[1:2], 0.0))
    with scope("barrier"):
        pl.semaphore_wait(barrier, DEVICES - 1)
        row_start(cnt_ref, cnt_ssem, cnt_rsem)
    with scope("fwd2"):
        forward(2)
        forward(3)
    with scope("zt"):
        loads["w2"].wait()
        zt = dot(w2_ref[...], act_ref[...].reshape(HID, TOK), ((0,), (0,)))
        zt = (xt_ref[...].astype(F32) + zt).astype(BF16)

    with scope("cls"):
        loads["heads"].wait()
        loads["lab"].wait()
        cls = lax.broadcasted_iota(jnp.int32, (CLS, TOK), 0)
        for t in range(TASKS):
            head = heads_ref[:, t, :]
            logits = dot(head, zt, ((1,), (0,)))
            ex = jnp.exp(logits - jnp.max(logits, axis=0, keepdims=True))
            prob = ex / jnp.sum(ex, axis=0, keepdims=True)
            onehot = jnp.where(lab_ref[t:t + 1, :] == cls, 1.0, 0.0)
            err = (mask_ref[t:t + 1, :].astype(F32) * (prob - onehot)).astype(BF16)
            dzt = dot(head, err, ((0,), (0,))).astype(BF16)
            dzt_ref[t] = dzt
            dz_ref[:, t * DIM:(t + 1) * DIM] = jnp.transpose(dzt)

    inv = []

    def wait_counts():
        with scope("cntwait"):
            row_all(cnt_ref, cnt_ssem, cnt_rsem).wait_recv()
            total = jnp.sum(cnt_ref[...], axis=0)
            inv.extend(1.0 / jnp.maximum(lane_pick(total, t), 1.0) for t in range(TASKS))

    @scoped
    def compute_b(k, *tasks):
        part = dot(act_ref[:, k].reshape(512, TOK), dz_ref[:, tasks[0] * DIM:(tasks[-1] + 1) * DIM], ((1,), (0,)))
        if not inv:
            wait_counts()
        for i, t in enumerate(tasks):
            scaled = (part[:, i * DIM:(i + 1) * DIM] * inv[t]).astype(BF16)
            send = bufs[1, k, t][0]
            for slot, first in enumerate(owners(PATH[1, k, t])):
                for n, j in enumerate(o for second in first for o in second):
                    send[slot, 16 * n:16 * (n + 1)] = scaled[16 * j:16 * (j + 1)]

    @scoped
    def compute_a(k, t):
        rows = slice(512 * k, 512 * (k + 1))
        back = dot(w2_ref[rows, :], dzt_ref[t], ((1,), (0,)))
        pre, cdf = pre_ref[rows, :], cdf_ref[rows, :]
        slope = cdf + (pre * cdf) * (1.0 - cdf) * (2.0 * GELU_C + (6.0 * GELU_C * GELU_A) * (pre * pre))
        dpre = (back * slope).astype(BF16)
        part = dot(xsel_ref[ORDER_OF[PATH[0, k, t]]], dpre, ((1,), (1,)))
        bufs[0, k, t][0][...] = (part * inv[t]).astype(BF16).reshape(4, 96, 512)

    def select_rows(r):
        xsel_ref[r] = dot(sel_ref[r], xt_ref[...], ((1,), (0,))).astype(BF16)

    def axes(piece, i):
        return (PATH[piece][0], "c") if i == 0 else axes_of(PATH[piece][i])

    def sent_on(piece, i):
        return 3 if i + 1 == len(PATH[piece]) else i

    def index_of(at, names):
        return sum(at[name] * 2 ** (len(names) - 1 - i) for i, name in enumerate(names))

    def send_stage(piece, i):
        send, recv = bufs[piece][2 * i:2 * i + 2]
        names = axes(piece, i)
        moves = list(itertools.product(range(2), repeat=len(names)))[1:]
        for p, move in reversed(list(enumerate(moves))):
            at = {name: flip(here[name], d) for name, d in zip(names, move)}
            remote(send.at[index_of(at, names)], recv.at[p], ssem.at[sent_on(piece, i)], rsem.at[NUMBER[piece], i],
                   peer(at)).start()

    def whole(ref, sem):
        return remote(ref, ref, sem, sem, others[0])

    @scoped
    def start(piece):
        send_stage(piece, 0)

    @scoped
    def advance(i, *pieces):
        for piece in pieces:
            advance_one(piece, i)

    def advance_one(piece, i):
        part, k, t = piece
        send, recv = bufs[piece][2 * i:2 * i + 2]
        whole(recv, rsem.at[NUMBER[piece], i]).wait_recv()
        terms = [send[index_of(here, axes(piece, i))].astype(F32)]
        terms += [recv[p].astype(F32) for p in range(recv.shape[0])]
        while len(terms) > 1:
            terms = [a + b for a, b in zip(terms[::2], terms[1::2])]
        tot = terms[0]
        if i + 1 < len(PATH[piece]):
            out = bufs[piece][2 * i + 2]
            if i == 1 and part == 0:
                count = tot.shape[0] // 12
                for q in range(count):
                    at = (q,) if count == 2 else (q // 2, q % 2)
                    top = tot[8 * q:8 * (q + 1)]
                    low = tot[8 * count + 4 * q:8 * count + 4 * (q + 1)]
                    out[at + (0,)] = top[:, :256]
                    out[at + (1,)] = top[:, 256:]
                    out[at + (2,)] = jnp.concatenate([low[:, :256], low[:, 256:]], axis=0)
            else:
                out[...] = tot.reshape(out.shape)
            send_stage(piece, i + 1)
        elif part == 0:
            for j in range(4):
                cols = slice(128 * (j % 2), 128 * (j % 2 + 1))
                gin_ref[t, pl.ds(4 * k + j, 8, stride=12), :] = tot[j // 2, :, cols]
                gin_ref[t, pl.ds(96 + 4 * k + j, 4, stride=12), :] = tot[2, 4 * (j // 2):4 * (j // 2 + 1), cols]
        else:
            for j in range(3):
                gout_ref[t, pl.ds(48 * k + j, 16, stride=3), :] = tot[:, 128 * j:128 * (j + 1)]

    compute_b(0, 0)
    start(Y[0])
    compute_b(0, 1)
    start(X[0])
    loads["sel"].wait()
    select_rows(ORDER_OF[PATH[Z[0]]])
    compute_a(0, 0)
    start(Z[0])
    compute_b(1, 0)
    start(Y[1])
    select_rows(ORDER_OF[PATH[X[1]]])
    compute_a(0, 1)
    start(X[1])
    compute_b(1, 1)
    start(Z[1])
    compute_a(1, 0)
    advance(0, Y[0], X[0])
    start(X[2])
    compute_b(2, 0, 1)
    start(Y[2])
    for r in range(len(ORDERS)):
        if r not in (ORDER_OF[PATH[Z[0]]], ORDER_OF[PATH[X[1]]]):
            select_rows(r)
    compute_a(1, 1)
    start(Z[2])
    advance(0, Y[1], X[1], Z[0])
    start(Y[3])
    compute_a(2, 0)
    advance(0, Z[1])
    start(X[3])
    compute_a(2, 1)
    start(Z[3])
    advance(1, X[0], Y[0])
    advance(0, Y[2], X[2])
    advance(2, X[0], Y[0])
    advance(1, X[1], Y[1])
    advance(1, Z[0], Z[1])
    advance(2, X[1], Y[1])
    advance(0, Y[3], X[3])
    advance(0, Z[2], Z[3])
    advance(1, X[2], Y[2])
    advance(2, Z[0], Z[1])
    advance(3, X[0], Y[0])
    advance(1, X[3], Y[3])
    advance(2, X[2], Y[2])
    advance(1, Z[2])
    advance(2, X[3], Y[3])
    advance(3, X[1], Y[1])
    advance(1, Z[3])
    advance(3, Z[0], Z[1])
    advance(3, X[2], Y[2])
    advance(2, Z[2])
    advance(3, X[3], Y[3])
    advance(2, Z[3])

    stores = [pltpu.make_async_copy(src, dst, out_sem.at[i])
              for i, (src, dst) in enumerate(((gin_ref, gin_hbm), (gout_ref, gout_hbm)))]
    with scope("gram"):
        row = jnp.zeros((1, 128), F32)
        for q, (s, t) in enumerate(((0, 0), (0, 1), (1, 1))):
            prod = gin_ref[s] * gin_ref[t] + gout_ref[s] * gout_ref[t]
            one = jnp.sum(jnp.sum(prod, axis=0, keepdims=True), axis=1, keepdims=True)
            row = jnp.where(lane == q, one, row)
        gram_ref[me] = row
    with scope("gramx"):
        row_start(gram_ref, gram_ssem, gram_rsem)
        stores[0].start()
        stores[1].start()
        for i in range(4):
            sent = [b[2 * j + 1] for piece, b in bufs.items() for j in range(len(PATH[piece])) if sent_on(piece, j) == i]
            nbytes = sum(math.prod(ref.shape) * (2 if i == 0 else 4) for ref in sent)
            whole(pre_ref.at[pl.ds(0, nbytes // (4 * TOK))], ssem.at[i]).wait_send()
        row_all(cnt_ref, cnt_ssem, cnt_rsem).wait_send()
        stores[0].wait()
        stores[1].wait()
        row_all(gram_ref, gram_ssem, gram_rsem).wait_recv()
    with scope("drain"):
        gram_out[...] = jnp.sum(gram_ref[...], axis=0)
        row_all(gram_ref, gram_ssem, gram_rsem).wait_send()


def combine(gram_ref, gin_hbm, gout_hbm, weights_ref, sum_in, sum_out, gin_ref, gout_ref, sem):
    loads = [pltpu.make_async_copy(src, dst, sem.at[i])
             for i, (src, dst) in enumerate(((gin_hbm, gin_ref), (gout_hbm, gout_ref)))]
    for load in loads:
        load.start()
    lane = lax.broadcasted_iota(jnp.int32, (1, 128), 1)
    m00, m01, m11 = [jnp.broadcast_to(jnp.sum(jnp.where(lane == q, gram_ref[...], 0.0), axis=1, keepdims=True), (1, 128))
                     for q in range(3)]
    scale = (m00 + m11) / 2.0
    w0 = jnp.full((1, 128), 0.5, F32)
    w1 = w0
    for _ in range(SOLVER_STEPS):
        r0 = w0 * jnp.exp(-(m00 * w0 + m01 * w1) / scale)
        r1 = w1 * jnp.exp(-(m01 * w0 + m11 * w1) / scale)
        norm = r0 + r1
        w0 = r0 / norm
        w1 = r1 / norm
    weights_ref[0] = w0[0, 0]
    weights_ref[1] = w1[0, 0]
    for load in loads:
        load.wait()
    sum_in[...] = w0 * gin_ref[0] + w1 * gin_ref[1]
    sum_out[...] = w0 * gout_ref[0] + w1 * gout_ref[1]


def solution(mesh):
    sel = select_matrices()

    def local_step(x_loc, w_in, w_out, task_heads, lab_loc, mask_loc):
        vmem = pl.BlockSpec(memory_space=pltpu.VMEM)
        hbm = pl.BlockSpec(memory_space=pl.ANY)
        dma = pltpu.SemaphoreType.DMA
        heads_t = jnp.transpose(task_heads, (2, 0, 1))
        args = (x_loc, w_in, w_out, heads_t, lab_loc, mask_loc, jnp.asarray(sel, BF16))
        piece = jax.ShapeDtypeStruct((144, 128), F32)
        outs = [jax.ShapeDtypeStruct((TASKS, 144, 128), F32)] * 2 + [jax.ShapeDtypeStruct((1, 128), F32)]
        scratch = [pltpu.VMEM(a.shape, a.dtype) for a in args] + [pltpu.VMEM(a.shape, a.dtype) for a in outs[:2]] + [
            pltpu.VMEM((DIM, TOK), BF16),
            pltpu.VMEM((32, CHUNKS, 16, TOK), BF16),
            pltpu.VMEM((HID, TOK), F32),
            pltpu.VMEM((HID, TOK), F32),
            pltpu.VMEM((len(ORDERS), DIM, TOK), BF16),
            pltpu.VMEM((TASKS, DIM, TOK), BF16),
            pltpu.VMEM((TOK, TASKS * DIM), BF16),
            pltpu.VMEM((DEVICES, 1, 128), F32),
            pltpu.VMEM((DEVICES, 1, 128), F32)]
        scratch += [pltpu.VMEM(*shape) for piece, path in PATH.items() for shape in buffers(piece[0], path)]
        scratch += [dma((len(args),)), dma((3,)), dma((len(PATH), 4)), dma((4,)), dma, dma, dma, dma]
        gin, gout, gram = pl.pallas_call(
            kernel,
            out_shape=outs,
            in_specs=[hbm] * len(args),
            out_specs=[hbm, hbm, vmem],
            scratch_shapes=scratch,
            compiler_params=pltpu.CompilerParams(collective_id=0, has_side_effects=True,
                                                 vmem_limit_bytes=66_900_000),
            name="step",
        )(*args)
        weights, grad_in, grad_out = pl.pallas_call(
            combine,
            out_shape=[jax.ShapeDtypeStruct((TASKS,), F32), piece, piece],
            in_specs=[vmem, hbm, hbm],
            out_specs=[pl.BlockSpec(memory_space=pltpu.SMEM), vmem, vmem],
            scratch_shapes=[pltpu.VMEM(outs[0].shape, F32), pltpu.VMEM(outs[1].shape, F32), dma((2,))],
            compiler_params=pltpu.CompilerParams(vmem_limit_bytes=66_900_000),
            name="combine",
        )(gram, gin, gout)
        return weights, grad_in.reshape(-1), grad_out.reshape(-1)

    return jax.shard_map(local_step, mesh=mesh,
                         in_specs=(P("data", None), P(), P(), P(), P(None, "data"), P(None, "data")),
                         out_specs=(P(), P("data"), P("data")), check_vma=False)
```

time: 60.8 us -> 61.2 us (level)
  no operation moved by 1% of the time
where the time goes in v4:
time: 61.2 us; the launch traced here: 61 us
  Pallas kernels  60.2 us (98%)
  between operations  0.8 us (1%)
    pallas_call x1, Pallas kernels, local_step(): pl.pallas_call(kernel, out_shape=outs, in_specs=[hbm] * len(args), out_sp...  57.9 us
    pallas_call x1, Pallas kernels, local_step(): pl.pallas_call(combine, out_shape=[jax.ShapeDtypeStruct((TASKS,), F32), p...  2.35 us

profile of v4, /device:TPU:0, one launch (start us, length us, event | category | flops | bytes accessed | tf_op | source)
XLA Modules:
  0.0 61.0 jit_solution(13946902808934922611)
XLA Ops:
  0.6 57.9 %step.1 = (f32[2,144,128]{2,1,0:T(8,128)}, f32[2,144,128]{2,1,0:T(8,128)}, f32[1,128]{1,0:T(1,128)}) custom-call(bf16[1024,384]{1,0:T(8,128)(2,1)} %x_hbm.1, bf16[384,1536]{1,0:T(8,128)(2,1)} %w1_hbm.1, bf16[1536,384]{1,0:T(8,128)(2,1)} %w2_hbm.1, bf16[10,2,384]{2,1,0:T(2,128)(2,1)} %bitcast.3, s32[2,1024]{1,0:T(2,128)} %lab_hbm.1, s32[2,1024]{1,0:T(2,128)} %mask_hbm.1, ...), custom_call_target="tpu_custom_call" | custom-call | tf_op jit(solution)/shard_map/step/pallas_call | solution.py:425
  58.5 2.3 %combine.1 = (f32[2]{0:T(128)}, f32[144,128]{1,0:T(8,128)}, f32[144,128]{1,0:T(8,128)}) custom-call(f32[1,128]{1,0:T(1,128)} %get-tuple-element.9.gram_ref, f32[2,144,128]{2,1,0:T(8,128)} %get-tuple-element.10.gin_hbm, f32[2,144,128]{2,1,0:T(8,128)} %get-tuple-element.11.gout_hbm), custom_call_target="tpu_custom_call" | custom-call | tf_op jit(solution)/shard_map/combine/pallas_call | solution.py:435

commit v5 on v4

--- a/solution.py
+++ b/solution.py
@@ -19,12 +19,13 @@
 GELU_A = 0.044715
 
 ROUTES = {"x": ("x", "y", "zl", "zh"), "y": ("y", "x", "zl", "zh"), "z": ("zl", "xy", "zh"),
-          "zyx": ("zl", "y", "x", "zh"), "zxy": ("zl", "x", "y", "zh")}
+          "x3": ("x", "y", "z"), "y3": ("y", "x", "z"), "zyx": ("zl", "y", "x", "zh"), "zxy": ("zl", "x", "y", "zh")}
+AXES = {"xy": ("y", "x"), "z": ("zl", "zh")}
 X = ((1, 0, 1), (0, 0, 1), (0, 1, 0), (0, 2, 0))
 Y = ((1, 0, 0), (1, 1, 0), (1, 2, 0), (1, 2, 1))
 Z = ((0, 0, 0), (1, 1, 1), (0, 1, 1), (0, 2, 1))
-PATH = dict.fromkeys(X, ROUTES["x"]) | dict.fromkeys(Y, ROUTES["y"]) | {
-    Z[0]: ROUTES["zyx"], Z[1]: ROUTES["zxy"], Z[2]: ROUTES["z"], Z[3]: ROUTES["z"]}
+CHOSEN = ("x", "x", "x3", "x3", "y", "y", "y3", "y3", "zyx", "zxy", "z", "z")
+PATH = {piece: ROUTES[name] for piece, name in zip(X + Y + Z, CHOSEN)}
 NUMBER = {piece: i for i, piece in enumerate(PATH)}
 COLS = (512, DIM)
 PLANE = (96, 128)
@@ -47,7 +48,7 @@
 
 
 def axes_of(stage):
-    return ("y", "x") if stage == "xy" else (stage,)
+    return AXES.get(stage, (stage,))
 
 
 def owners(path):
@@ -79,11 +80,13 @@
 
 
 def buffers(part, path):
-    rows, cols, fan = PLANE[part], COLS[part], 2 ** len(axes_of(path[1]))
+    rows, cols = PLANE[part], COLS[part]
+    fans = [2 ** len(axes_of(stage)) for stage in path]
     shapes = [((4, rows, cols), BF16), ((3, rows, cols), BF16),
-              ((fan, rows // fan, cols), F32), ((fan - 1, rows // fan, cols), F32)]
-    for left in range(len(path) - 3, -1, -1):
-        shapes += [((2,) * (left + 1) + TILE[part], F32), ((1,) + (2,) * left + TILE[part], F32)]
+              ((fans[1], rows // fans[1], cols), F32), ((fans[1] - 1, rows // fans[1], cols), F32)]
+    for i in range(2, len(path)):
+        later = tuple(fans[i + 1:])
+        shapes += [((fans[i],) + later + TILE[part], F32), ((fans[i] - 1,) + later + TILE[part], F32)]
     return shapes
 
 
@@ -101,7 +104,7 @@
 def kernel(x_hbm, w1_hbm, w2_hbm, heads_hbm, lab_hbm, mask_hbm, sel_hbm,
            gin_hbm, gout_hbm, gram_out,
            x_ref, w1_ref, w2_ref, heads_ref, lab_ref, mask_ref, sel_ref,
-           gin_ref, gout_ref, xt_ref, act_ref, pre_ref, cdf_ref, xsel_ref, dzt_ref, dz_ref, cnt_ref, gram_ref, *rest):
+           gin_ref, gout_ref, xt_ref, act_ref, pre_ref, cdf_ref, xsel_ref, dzt_ref, dz_ref, err_ref, cnt_ref, gram_ref, *rest):
     rest = list(rest)
     bufs = {piece: [rest.pop(0) for _ in range(2 * len(path))] for piece, path in PATH.items()}
     in_sem, out_sem, rsem, ssem, cnt_ssem, cnt_rsem, gram_ssem, gram_rsem = rest
@@ -186,17 +189,22 @@
     with scope("cls"):
         loads["heads"].wait()
         loads["lab"].wait()
-        cls = lax.broadcasted_iota(jnp.int32, (CLS, TOK), 0)
+        pad = jnp.zeros((16 - CLS, DIM), BF16)
+        heads = jnp.concatenate([heads_ref[:, 0, :], pad, heads_ref[:, 1, :], pad], axis=0)
+        logits = dot(heads, zt, ((1,), (0,)))
+        cls = lax.broadcasted_iota(jnp.int32, (16, TOK), 0)
         for t in range(TASKS):
-            head = heads_ref[:, t, :]
-            logits = dot(head, zt, ((1,), (0,)))
-            ex = jnp.exp(logits - jnp.max(logits, axis=0, keepdims=True))
+            score = jnp.where(cls < CLS, logits[16 * t:16 * (t + 1)], -jnp.inf)
+            ex = jnp.exp(score - jnp.max(score, axis=0, keepdims=True))
             prob = ex / jnp.sum(ex, axis=0, keepdims=True)
             onehot = jnp.where(lab_ref[t:t + 1, :] == cls, 1.0, 0.0)
-            err = (mask_ref[t:t + 1, :].astype(F32) * (prob - onehot)).astype(BF16)
-            dzt = dot(head, err, ((0,), (0,))).astype(BF16)
-            dzt_ref[t] = dzt
-            dz_ref[:, t * DIM:(t + 1) * DIM] = jnp.transpose(dzt)
+            err_ref[t] = (mask_ref[t:t + 1, :].astype(F32) * (prob - onehot)).astype(BF16)
+            head = heads[16 * t:16 * (t + 1)]
+            dz_ref[:, t * DIM:(t + 1) * DIM] = dot(err_ref[t], head, ((0,), (0,))).astype(BF16)
+
+    def compute_dzt():
+        for t in range(TASKS):
+            dzt_ref[t] = dot(heads[16 * t:16 * (t + 1)], err_ref[t], ((0,), (0,))).astype(BF16)
 
     inv = []
 
@@ -275,7 +283,7 @@
             if i == 1 and part == 0:
                 count = tot.shape[0] // 12
                 for q in range(count):
-                    at = (q,) if count == 2 else (q // 2, q % 2)
+                    at = (q,) if out.shape[0] == count else (q // 2, q % 2)
                     top = tot[8 * q:8 * (q + 1)]
                     low = tot[8 * count + 4 * q:8 * count + 4 * (q + 1)]
                     out[at + (0,)] = top[:, :256]
@@ -293,60 +301,63 @@
             for j in range(3):
                 gout_ref[t, pl.ds(48 * k + j, 16, stride=3), :] = tot[:, 128 * j:128 * (j + 1)]
 
+    compute_b(0, 1)
+    start(X[0])
     compute_b(0, 0)
     start(Y[0])
-    compute_b(0, 1)
-    start(X[0])
+    compute_b(1, 1)
+    start(Z[1])
+    compute_b(2, 0, 1)
     loads["sel"].wait()
-    select_rows(ORDER_OF[PATH[Z[0]]])
+    select_rows(0)
+    compute_dzt()
+    compute_a(1, 0)
+    start(Y[2])
+    start(X[2])
+    select_rows(2)
+    compute_a(1, 1)
+    select_rows(1)
+    start(Z[2])
+    compute_a(0, 1)
+    advance(0, X[0])
+    compute_b(1, 0)
+    advance(0, Y[0], Z[1])
     compute_a(0, 0)
     start(Z[0])
-    compute_b(1, 0)
-    start(Y[1])
-    select_rows(ORDER_OF[PATH[X[1]]])
-    compute_a(0, 1)
-    start(X[1])
-    compute_b(1, 1)
-    start(Z[1])
-    compute_a(1, 0)
-    advance(0, Y[0], X[0])
-    start(X[2])
-    compute_b(2, 0, 1)
-    start(Y[2])
-    for r in range(len(ORDERS)):
-        if r not in (ORDER_OF[PATH[Z[0]]], ORDER_OF[PATH[X[1]]]):
-            select_rows(r)
-    compute_a(1, 1)
-    start(Z[2])
-    advance(0, Y[1], X[1], Z[0])
     start(Y[3])
-    compute_a(2, 0)
-    advance(0, Z[1])
-    start(X[3])
+    advance(0, Y[2])
     compute_a(2, 1)
     start(Z[3])
-    advance(1, X[0], Y[0])
-    advance(0, Y[2], X[2])
-    advance(2, X[0], Y[0])
-    advance(1, X[1], Y[1])
-    advance(1, Z[0], Z[1])
-    advance(2, X[1], Y[1])
-    advance(0, Y[3], X[3])
-    advance(0, Z[2], Z[3])
-    advance(1, X[2], Y[2])
-    advance(2, Z[0], Z[1])
-    advance(3, X[0], Y[0])
-    advance(1, X[3], Y[3])
-    advance(2, X[2], Y[2])
+    compute_a(2, 0)
+    start(X[3])
+    advance(0, X[2])
+    start(Y[1])
+    advance(0, Y[3])
+    advance(1, Y[2], X[0], X[2])
+    advance(0, X[3], Z[0])
+    start(X[1])
+    advance(1, Y[0])
+    advance(2, X[0])
+    advance(1, Y[3], Z[1])
+    advance(0, Y[1])
+    advance(2, X[2], Y[0])
+    advance(0, X[1])
+    advance(1, X[3], Z[0])
+    advance(0, Z[3])
+    advance(1, Y[1])
+    advance(2, Z[1], Z[0])
+    advance(0, Z[2])
+    advance(1, X[1])
+    advance(3, X[0])
+    advance(2, Y[1])
+    advance(1, Z[3])
+    advance(3, Z[0])
+    advance(2, Y[2], X[1])
     advance(1, Z[2])
-    advance(2, X[3], Y[3])
-    advance(3, X[1], Y[1])
-    advance(1, Z[3])
-    advance(3, Z[0], Z[1])
-    advance(3, X[2], Y[2])
-    advance(2, Z[2])
-    advance(3, X[3], Y[3])
-    advance(2, Z[3])
+    advance(3, Y[0], X[1])
+    advance(2, X[3])
+    advance(3, Y[1], Z[1])
+    advance(2, Z[3], Y[3], Z[2])
 
     stores = [pltpu.make_async_copy(src, dst, out_sem.at[i])
               for i, (src, dst) in enumerate(((gin_ref, gin_hbm), (gout_ref, gout_hbm)))]
@@ -418,6 +429,7 @@
             pltpu.VMEM((len(ORDERS), DIM, TOK), BF16),
             pltpu.VMEM((TASKS, DIM, TOK), BF16),
             pltpu.VMEM((TOK, TASKS * DIM), BF16),
+            pltpu.VMEM((TASKS, 16, TOK), BF16),
             pltpu.VMEM((DEVICES, 1, 128), F32),
             pltpu.VMEM((DEVICES, 1, 128), F32)]
         scratch += [pltpu.VMEM(*shape) for piece, path in PATH.items() for shape in buffers(piece[0], path)]

time: 61.2 us -> 61.4 us (level)
  no operation moved by 1% of the time
where the time goes in v5:
time: 61.4 us; the launch traced here: 61.3 us
  Pallas kernels  60.5 us (99%)
  between operations  0.8 us (1%)
    pallas_call x1, Pallas kernels, local_step(): pl.pallas_call(kernel, out_shape=outs, in_specs=[hbm] * len(args), out_sp...  58.1 us
    pallas_call x1, Pallas kernels, local_step(): pl.pallas_call(combine, out_shape=[jax.ShapeDtypeStruct((TASKS,), F32), p...  2.35 us

profile of v5, /device:TPU:0, one launch (start us, length us, event | category | flops | bytes accessed | tf_op | source)
XLA Modules:
  0.0 61.3 jit_solution(5241236432065509026)
XLA Ops:
  0.6 58.1 %step.1 = (f32[2,144,128]{2,1,0:T(8,128)}, f32[2,144,128]{2,1,0:T(8,128)}, f32[1,128]{1,0:T(1,128)}) custom-call(bf16[1024,384]{1,0:T(8,128)(2,1)} %x_hbm.1, bf16[384,1536]{1,0:T(8,128)(2,1)} %w1_hbm.1, bf16[1536,384]{1,0:T(8,128)(2,1)} %w2_hbm.1, bf16[10,2,384]{2,1,0:T(2,128)(2,1)} %bitcast.3, s32[2,1024]{1,0:T(2,128)} %lab_hbm.1, s32[2,1024]{1,0:T(2,128)} %mask_hbm.1, ...), custom_call_target="tpu_custom_call" | custom-call | tf_op jit(solution)/shard_map/step/pallas_call | solution.py:437
  58.7 2.3 %combine.1 = (f32[2]{0:T(128)}, f32[144,128]{1,0:T(8,128)}, f32[144,128]{1,0:T(8,128)}) custom-call(f32[1,128]{1,0:T(1,128)} %get-tuple-element.9.gram_ref, f32[2,144,128]{2,1,0:T(8,128)} %get-tuple-element.10.gin_hbm, f32[2,144,128]{2,1,0:T(8,128)} %get-tuple-element.11.gout_hbm), custom_call_target="tpu_custom_call" | custom-call | tf_op jit(solution)/shard_map/combine/pallas_call | solution.py:447

commit v6 on v5

--- a/solution.py
+++ b/solution.py
@@ -19,12 +19,12 @@
 GELU_A = 0.044715
 
 ROUTES = {"x": ("x", "y", "zl", "zh"), "y": ("y", "x", "zl", "zh"), "z": ("zl", "xy", "zh"),
-          "x3": ("x", "y", "z"), "y3": ("y", "x", "z"), "zyx": ("zl", "y", "x", "zh"), "zxy": ("zl", "x", "y", "zh")}
+          "x3": ("x", "y", "z"), "y3": ("y", "x", "z"), "zh": ("zl", "zh", "xy")}
 AXES = {"xy": ("y", "x"), "z": ("zl", "zh")}
 X = ((1, 0, 1), (0, 0, 1), (0, 1, 0), (0, 2, 0))
 Y = ((1, 0, 0), (1, 1, 0), (1, 2, 0), (1, 2, 1))
 Z = ((0, 0, 0), (1, 1, 1), (0, 1, 1), (0, 2, 1))
-CHOSEN = ("x", "x", "x3", "x3", "y", "y", "y3", "y3", "zyx", "zxy", "z", "z")
+CHOSEN = ("x3", "x3", "x", "x", "y3", "y3", "y", "y", "z", "zh", "z", "z")
 PATH = {piece: ROUTES[name] for piece, name in zip(X + Y + Z, CHOSEN)}
 NUMBER = {piece: i for i, piece in enumerate(PATH)}
 COLS = (512, DIM)
@@ -104,7 +104,7 @@
 def kernel(x_hbm, w1_hbm, w2_hbm, heads_hbm, lab_hbm, mask_hbm, sel_hbm,
            gin_hbm, gout_hbm, gram_out,
            x_ref, w1_ref, w2_ref, heads_ref, lab_ref, mask_ref, sel_ref,
-           gin_ref, gout_ref, xt_ref, act_ref, pre_ref, cdf_ref, xsel_ref, dzt_ref, dz_ref, err_ref, cnt_ref, gram_ref, *rest):
+           gin_ref, gout_ref, xt_ref, act_ref, pre_ref, cdf_ref, xsel_ref, dz_ref, err_ref, cnt_ref, gram_ref, *rest):
     rest = list(rest)
     bufs = {piece: [rest.pop(0) for _ in range(2 * len(path))] for piece, path in PATH.items()}
     in_sem, out_sem, rsem, ssem, cnt_ssem, cnt_rsem, gram_ssem, gram_rsem = rest
@@ -202,10 +202,6 @@
             head = heads[16 * t:16 * (t + 1)]
             dz_ref[:, t * DIM:(t + 1) * DIM] = dot(err_ref[t], head, ((0,), (0,))).astype(BF16)
 
-    def compute_dzt():
-        for t in range(TASKS):
-            dzt_ref[t] = dot(heads[16 * t:16 * (t + 1)], err_ref[t], ((0,), (0,))).astype(BF16)
-
     inv = []
 
     def wait_counts():
@@ -229,7 +225,7 @@
     @scoped
     def compute_a(k, t):
         rows = slice(512 * k, 512 * (k + 1))
-        back = dot(w2_ref[rows, :], dzt_ref[t], ((1,), (0,)))
+        back = dot(w2_ref[rows, :], dz_ref[:, t * DIM:(t + 1) * DIM], ((1,), (1,)))
         pre, cdf = pre_ref[rows, :], cdf_ref[rows, :]
         slope = cdf + (pre * cdf) * (1.0 - cdf) * (2.0 * GELU_C + (6.0 * GELU_C * GELU_A) * (pre * pre))
         dpre = (back * slope).astype(BF16)
@@ -301,63 +297,60 @@
             for j in range(3):
                 gout_ref[t, pl.ds(48 * k + j, 16, stride=3), :] = tot[:, 128 * j:128 * (j + 1)]
 
+    compute_b(1, 1)
+    start(Z[1])
     compute_b(0, 1)
     start(X[0])
+    compute_b(1, 0)
+    start(Y[1])
+    loads["sel"].wait()
+    select_rows(1)
+    compute_a(0, 0)
+    select_rows(0)
+    start(Z[0])
+    compute_a(0, 1)
+    start(X[1])
     compute_b(0, 0)
     start(Y[0])
-    compute_b(1, 1)
-    start(Z[1])
     compute_b(2, 0, 1)
-    loads["sel"].wait()
-    select_rows(0)
-    compute_dzt()
+    compute_a(2, 1)
+    start(Y[2])
+    advance(0, Z[1], Y[1])
     compute_a(1, 0)
-    start(Y[2])
     start(X[2])
-    select_rows(2)
+    start(Z[3])
+    advance(0, X[0])
+    compute_a(2, 0)
+    advance(1, Y[1])
     compute_a(1, 1)
-    select_rows(1)
+    advance(0, Y[0], Y[2])
     start(Z[2])
-    compute_a(0, 1)
-    advance(0, X[0])
-    compute_b(1, 0)
-    advance(0, Y[0], Z[1])
-    compute_a(0, 0)
-    start(Z[0])
     start(Y[3])
-    advance(0, Y[2])
-    compute_a(2, 1)
-    start(Z[3])
-    compute_a(2, 0)
     start(X[3])
-    advance(0, X[2])
-    start(Y[1])
+    advance(1, Y[0], X[0])
+    advance(0, X[1])
+    advance(2, Y[1])
     advance(0, Y[3])
-    advance(1, Y[2], X[0], X[2])
-    advance(0, X[3], Z[0])
-    start(X[1])
-    advance(1, Y[0])
-    advance(2, X[0])
-    advance(1, Y[3], Z[1])
-    advance(0, Y[1])
-    advance(2, X[2], Y[0])
-    advance(0, X[1])
-    advance(1, X[3], Z[0])
-    advance(0, Z[3])
-    advance(1, Y[1])
-    advance(2, Z[1], Z[0])
-    advance(0, Z[2])
-    advance(1, X[1])
-    advance(3, X[0])
-    advance(2, Y[1])
-    advance(1, Z[3])
-    advance(3, Z[0])
-    advance(2, Y[2], X[1])
-    advance(1, Z[2])
-    advance(3, Y[0], X[1])
+    advance(1, Y[2])
+    advance(0, X[2], Z[3])
+    advance(1, X[1], X[2])
+    advance(0, X[3], Z[2], Z[0])
+    advance(2, Y[2], Y[0])
+    advance(1, Y[3])
+    advance(2, X[2])
+    advance(1, Z[3], X[3])
+    advance(2, Y[3])
+    advance(1, Z[1], Z[2])
     advance(2, X[3])
-    advance(3, Y[1], Z[1])
-    advance(2, Z[3], Y[3], Z[2])
+    advance(3, X[2])
+    advance(2, Z[3])
+    advance(1, Z[0])
+    advance(3, Y[3])
+    advance(2, X[1])
+    advance(3, X[3])
+    advance(2, X[0], Z[1])
+    advance(3, Y[2])
+    advance(2, Z[2], Z[0])
 
     stores = [pltpu.make_async_copy(src, dst, out_sem.at[i])
               for i, (src, dst) in enumerate(((gin_ref, gin_hbm), (gout_ref, gout_hbm)))]
@@ -375,7 +368,8 @@
         for i in range(4):
             sent = [b[2 * j + 1] for piece, b in bufs.items() for j in range(len(PATH[piece])) if sent_on(piece, j) == i]
             nbytes = sum(math.prod(ref.shape) * (2 if i == 0 else 4) for ref in sent)
-            whole(pre_ref.at[pl.ds(0, nbytes // (4 * TOK))], ssem.at[i]).wait_send()
+            width = next(w for w in (1024, 512, 256) if nbytes // (4 * w) % 8 == 0)
+            whole(pre_ref.at[pl.ds(0, nbytes // (4 * width)), pl.ds(0, width)], ssem.at[i]).wait_send()
         row_all(cnt_ref, cnt_ssem, cnt_rsem).wait_send()
         stores[0].wait()
         stores[1].wait()
@@ -427,7 +421,6 @@
             pltpu.VMEM((HID, TOK), F32),
             pltpu.VMEM((HID, TOK), F32),
             pltpu.VMEM((len(ORDERS), DIM, TOK), BF16),
-            pltpu.VMEM((TASKS, DIM, TOK), BF16),
             pltpu.VMEM((TOK, TASKS * DIM), BF16),
             pltpu.VMEM((TASKS, 16, TOK), BF16),
             pltpu.VMEM((DEVICES, 1, 128), F32),

time: 61.4 us -> 61.1 us (level)
  no operation moved by 1% of the time
where the time goes in v6:
time: 61.1 us; the launch traced here: 60.9 us
  Pallas kernels  60.3 us (99%)
  between operations  0.64 us (1%)
    pallas_call x1, Pallas kernels, local_step(): pl.pallas_call(kernel, out_shape=outs, in_specs=[hbm] * len(args), out_sp...  57.9 us
    pallas_call x1, Pallas kernels, local_step(): pl.pallas_call(combine, out_shape=[jax.ShapeDtypeStruct((TASKS,), F32), p...  2.35 us

profile of v6, /device:TPU:0, one launch (start us, length us, event | category | flops | bytes accessed | tf_op | source)
XLA Modules:
  0.0 60.9 jit_solution(4774103615294835072)
XLA Ops:
  0.6 57.9 %step.1 = (f32[2,144,128]{2,1,0:T(8,128)}, f32[2,144,128]{2,1,0:T(8,128)}, f32[1,128]{1,0:T(1,128)}) custom-call(bf16[1024,384]{1,0:T(8,128)(2,1)} %x_hbm.1, bf16[384,1536]{1,0:T(8,128)(2,1)} %w1_hbm.1, bf16[1536,384]{1,0:T(8,128)(2,1)} %w2_hbm.1, bf16[10,2,384]{2,1,0:T(2,128)(2,1)} %bitcast.3, s32[2,1024]{1,0:T(2,128)} %lab_hbm.1, s32[2,1024]{1,0:T(2,128)} %mask_hbm.1, ...), custom_call_target="tpu_custom_call" | custom-call | tf_op jit(solution)/shard_map/step/pallas_call | solution.py:430
  58.6 2.3 %combine.1 = (f32[2]{0:T(128)}, f32[144,128]{1,0:T(8,128)}, f32[144,128]{1,0:T(8,128)}) custom-call(f32[1,128]{1,0:T(1,128)} %get-tuple-element.9.gram_ref, f32[2,144,128]{2,1,0:T(8,128)} %get-tuple-element.10.gin_hbm, f32[2,144,128]{2,1,0:T(8,128)} %get-tuple-element.11.gout_hbm), custom_call_target="tpu_custom_call" | custom-call | tf_op jit(solution)/shard_map/combine/pallas_call | solution.py:440

commit v7 on v6

--- a/solution.py
+++ b/solution.py
@@ -19,7 +19,8 @@
 GELU_A = 0.044715
 
 ROUTES = {"x": ("x", "y", "zl", "zh"), "y": ("y", "x", "zl", "zh"), "z": ("zl", "xy", "zh"),
-          "x3": ("x", "y", "z"), "y3": ("y", "x", "z"), "zh": ("zl", "zh", "xy")}
+          "x3": ("x", "y", "z"), "y3": ("y", "x", "z"), "zh": ("zl", "zh", "xy"),
+          "zyx": ("zl", "y", "x", "zh"), "zxy": ("zl", "x", "y", "zh")}
 AXES = {"xy": ("y", "x"), "z": ("zl", "zh")}
 X = ((1, 0, 1), (0, 0, 1), (0, 1, 0), (0, 2, 0))
 Y = ((1, 0, 0), (1, 1, 0), (1, 2, 0), (1, 2, 1))
@@ -297,60 +298,59 @@
             for j in range(3):
                 gout_ref[t, pl.ds(48 * k + j, 16, stride=3), :] = tot[:, 128 * j:128 * (j + 1)]
 
+    compute_b(0, 0)
+    start(Y[0])
+    compute_b(0, 1)
+    start(X[0])
     compute_b(1, 1)
     start(Z[1])
-    compute_b(0, 1)
-    start(X[0])
+    compute_b(2, 0, 1)
+    loads["sel"].wait()
+    select_rows(0)
+    start(Y[2])
+    compute_a(2, 0)
+    start(X[3])
+    select_rows(1)
+    compute_a(1, 1)
+    start(Z[2])
+    compute_a(2, 1)
     compute_b(1, 0)
+    advance(0, Y[0], X[0])
+    compute_a(0, 1)
+    advance(0, Z[1])
     start(Y[1])
-    loads["sel"].wait()
-    select_rows(1)
+    start(X[1])
+    start(Z[3])
     compute_a(0, 0)
-    select_rows(0)
+    advance(0, Y[2])
+    start(Y[3])
+    compute_a(1, 0)
+    advance(1, Y[0])
+    start(X[2])
     start(Z[0])
-    compute_a(0, 1)
-    start(X[1])
-    compute_b(0, 0)
-    start(Y[0])
-    compute_b(2, 0, 1)
-    compute_a(2, 1)
-    start(Y[2])
-    advance(0, Z[1], Y[1])
-    compute_a(1, 0)
-    start(X[2])
-    start(Z[3])
-    advance(0, X[0])
-    compute_a(2, 0)
+    advance(0, Y[1], X[1])
+    advance(1, X[0])
+    advance(0, X[3])
+    advance(1, Y[2])
+    advance(0, Y[3], Z[3])
+    advance(1, X[1])
+    advance(0, X[2], Z[0])
+    advance(1, X[3])
+    advance(0, Z[2])
     advance(1, Y[1])
-    compute_a(1, 1)
-    advance(0, Y[0], Y[2])
-    start(Z[2])
-    start(Y[3])
-    start(X[3])
-    advance(1, Y[0], X[0])
-    advance(0, X[1])
-    advance(2, Y[1])
-    advance(0, Y[3])
-    advance(1, Y[2])
-    advance(0, X[2], Z[3])
-    advance(1, X[1], X[2])
-    advance(0, X[3], Z[2], Z[0])
-    advance(2, Y[2], Y[0])
+    advance(2, Y[2])
     advance(1, Y[3])
-    advance(2, X[2])
-    advance(1, Z[3], X[3])
-    advance(2, Y[3])
-    advance(1, Z[1], Z[2])
-    advance(2, X[3])
-    advance(3, X[2])
-    advance(2, Z[3])
-    advance(1, Z[0])
+    advance(2, X[0], X[3])
+    advance(1, X[2], Z[3], Z[1], Z[0])
+    advance(2, Y[3], X[2], Y[0])
+    advance(1, Z[2])
+    advance(2, Z[3], Y[1], Z[1])
+    advance(3, X[2], X[3])
+    advance(2, Z[0])
     advance(3, Y[3])
     advance(2, X[1])
-    advance(3, X[3])
-    advance(2, X[0], Z[1])
     advance(3, Y[2])
-    advance(2, Z[2], Z[0])
+    advance(2, Z[2])
 
     stores = [pltpu.make_async_copy(src, dst, out_sem.at[i])
               for i, (src, dst) in enumerate(((gin_ref, gin_hbm), (gout_ref, gout_hbm)))]

time: 61.1 us -> 59.2 us (0.969)
  Pallas kernels: 60.3 us -> 58.2 us
    pallas_call x1, Pallas kernels: 57.9 us -> 55.9 us  [local_step(): pl.pallas_call(kernel, out_shape=outs, in_specs=[hbm] * len(args), out_sp...]
where the time goes in v7:
time: 59.2 us; the launch traced here: 59 us
  Pallas kernels  58.2 us (98%)
  between operations  0.8 us (1%)
    pallas_call x1, Pallas kernels, local_step(): pl.pallas_call(kernel, out_shape=outs, in_specs=[hbm] * len(args), out_sp...  55.9 us
    pallas_call x1, Pallas kernels, local_step(): pl.pallas_call(combine, out_shape=[jax.ShapeDtypeStruct((TASKS,), F32), p...  2.35 us

profile of v7, /device:TPU:0, one launch (start us, length us, event | category | flops | bytes accessed | tf_op | source)
XLA Modules:
  0.0 59.0 jit_solution(9427860892428190563)
XLA Ops:
  0.6 55.9 %step.1 = (f32[2,144,128]{2,1,0:T(8,128)}, f32[2,144,128]{2,1,0:T(8,128)}, f32[1,128]{1,0:T(1,128)}) custom-call(bf16[1024,384]{1,0:T(8,128)(2,1)} %x_hbm.1, bf16[384,1536]{1,0:T(8,128)(2,1)} %w1_hbm.1, bf16[1536,384]{1,0:T(8,128)(2,1)} %w2_hbm.1, bf16[10,2,384]{2,1,0:T(2,128)(2,1)} %bitcast.3, s32[2,1024]{1,0:T(2,128)} %lab_hbm.1, s32[2,1024]{1,0:T(2,128)} %mask_hbm.1, ...), custom_call_target="tpu_custom_call" | custom-call | tf_op jit(solution)/shard_map/step/pallas_call | solution.py:430
  56.5 2.3 %combine.1 = (f32[2]{0:T(128)}, f32[144,128]{1,0:T(8,128)}, f32[144,128]{1,0:T(8,128)}) custom-call(f32[1,128]{1,0:T(1,128)} %get-tuple-element.9.gram_ref, f32[2,144,128]{2,1,0:T(8,128)} %get-tuple-element.10.gin_hbm, f32[2,144,128]{2,1,0:T(8,128)} %get-tuple-element.11.gout_hbm), custom_call_target="tpu_custom_call" | custom-call | tf_op jit(solution)/shard_map/combine/pallas_call | solution.py:440

commit v8 on v7

--- a/solution.py
+++ b/solution.py
@@ -103,9 +103,9 @@
 
 
 def kernel(x_hbm, w1_hbm, w2_hbm, heads_hbm, lab_hbm, mask_hbm, sel_hbm,
-           gin_hbm, gout_hbm, gram_out,
+           gin_hbm, gout_hbm, gram_hbm,
            x_ref, w1_ref, w2_ref, heads_ref, lab_ref, mask_ref, sel_ref,
-           gin_ref, gout_ref, xt_ref, act_ref, pre_ref, cdf_ref, xsel_ref, dz_ref, err_ref, cnt_ref, gram_ref, *rest):
+           gin_ref, gout_ref, gram_out, xt_ref, act_ref, pre_ref, cdf_ref, xsel_ref, dz_ref, err_ref, cnt_ref, gram_ref, *rest):
     rest = list(rest)
     bufs = {piece: [rest.pop(0) for _ in range(2 * len(path))] for piece, path in PATH.items()}
     in_sem, out_sem, rsem, ssem, cnt_ssem, cnt_rsem, gram_ssem, gram_rsem = rest
@@ -353,7 +353,7 @@
     advance(2, Z[2])
 
     stores = [pltpu.make_async_copy(src, dst, out_sem.at[i])
-              for i, (src, dst) in enumerate(((gin_ref, gin_hbm), (gout_ref, gout_hbm)))]
+              for i, (src, dst) in enumerate(((gin_ref, gin_hbm), (gout_ref, gout_hbm), (gram_out, gram_hbm)))]
     with scope("gram"):
         row = jnp.zeros((1, 128), F32)
         for q, (s, t) in enumerate(((0, 0), (0, 1), (1, 1))):
@@ -376,14 +376,17 @@
         row_all(gram_ref, gram_ssem, gram_rsem).wait_recv()
     with scope("drain"):
         gram_out[...] = jnp.sum(gram_ref[...], axis=0)
+        stores[2].start()
         row_all(gram_ref, gram_ssem, gram_rsem).wait_send()
-
-
-def combine(gram_ref, gin_hbm, gout_hbm, weights_ref, sum_in, sum_out, gin_ref, gout_ref, sem):
+        stores[2].wait()
+
+
+def combine(gram_hbm, gin_hbm, gout_hbm, weights_ref, sum_in, sum_out, gram_ref, gin_ref, gout_ref, sem):
     loads = [pltpu.make_async_copy(src, dst, sem.at[i])
-             for i, (src, dst) in enumerate(((gin_hbm, gin_ref), (gout_hbm, gout_ref)))]
+             for i, (src, dst) in enumerate(((gram_hbm, gram_ref), (gin_hbm, gin_ref), (gout_hbm, gout_ref)))]
     for load in loads:
         load.start()
+    loads[0].wait()
     lane = lax.broadcasted_iota(jnp.int32, (1, 128), 1)
     m00, m01, m11 = [jnp.broadcast_to(jnp.sum(jnp.where(lane == q, gram_ref[...], 0.0), axis=1, keepdims=True), (1, 128))
                      for q in range(3)]
@@ -398,8 +401,8 @@
         w1 = r1 / norm
     weights_ref[0] = w0[0, 0]
     weights_ref[1] = w1[0, 0]
-    for load in loads:
-        load.wait()
+    loads[1].wait()
+    loads[2].wait()
     sum_in[...] = w0 * gin_ref[0] + w1 * gin_ref[1]
     sum_out[...] = w0 * gout_ref[0] + w1 * gout_ref[1]
 
@@ -415,7 +418,7 @@
         args = (x_loc, w_in, w_out, heads_t, lab_loc, mask_loc, jnp.asarray(sel, BF16))
         piece = jax.ShapeDtypeStruct((144, 128), F32)
         outs = [jax.ShapeDtypeStruct((TASKS, 144, 128), F32)] * 2 + [jax.ShapeDtypeStruct((1, 128), F32)]
-        scratch = [pltpu.VMEM(a.shape, a.dtype) for a in args] + [pltpu.VMEM(a.shape, a.dtype) for a in outs[:2]] + [
+        scratch = [pltpu.VMEM(a.shape, a.dtype) for a in args] + [pltpu.VMEM(a.shape, a.dtype) for a in outs] + [
             pltpu.VMEM((DIM, TOK), BF16),
             pltpu.VMEM((32, CHUNKS, 16, TOK), BF16),
             pltpu.VMEM((HID, TOK), F32),
@@ -431,7 +434,7 @@
             kernel,
             out_shape=outs,
             in_specs=[hbm] * len(args),
-            out_specs=[hbm, hbm, vmem],
+            out_specs=[hbm] * 3,
             scratch_shapes=scratch,
             compiler_params=pltpu.CompilerParams(collective_id=0, has_side_effects=True,
                                                  vmem_limit_bytes=66_900_000),
@@ -440,9 +443,10 @@
         weights, grad_in, grad_out = pl.pallas_call(
             combine,
             out_shape=[jax.ShapeDtypeStruct((TASKS,), F32), piece, piece],
-            in_specs=[vmem, hbm, hbm],
+            in_specs=[hbm] * 3,
             out_specs=[pl.BlockSpec(memory_space=pltpu.SMEM), vmem, vmem],
-            scratch_shapes=[pltpu.VMEM(outs[0].shape, F32), pltpu.VMEM(outs[1].shape, F32), dma((2,))],
+            scratch_shapes=[pltpu.VMEM(outs[2].shape, F32), pltpu.VMEM(outs[0].shape, F32),
+                            pltpu.VMEM(outs[1].shape, F32), dma((3,))],
             compiler_params=pltpu.CompilerParams(vmem_limit_bytes=66_900_000),
             name="combine",
         )(gram, gin, gout)

time: 59.2 us -> 58.8 us (level)
  no operation moved by 1% of the time
where the time goes in v8:
time: 58.8 us; the launch traced here: 58.6 us
  Pallas kernels  57.8 us (98%)
  between operations  0.8 us (1%)
    pallas_call x1, Pallas kernels, local_step(): pl.pallas_call(kernel, out_shape=outs, in_specs=[hbm] * len(args), out_sp...  55.9 us
    pallas_call x1, Pallas kernels, local_step(): pl.pallas_call(combine, out_shape=[jax.ShapeDtypeStruct((TASKS,), F32), p...  1.91 us

profile of v8, /device:TPU:0, one launch (start us, length us, event | category | flops | bytes accessed | tf_op | source)
XLA Modules:
  0.0 58.6 jit_solution(15031347727117907864)
XLA Ops:
  0.6 55.9 %step.1 = (f32[2,144,128]{2,1,0:T(8,128)}, f32[2,144,128]{2,1,0:T(8,128)}, f32[1,128]{1,0:T(1,128)}) custom-call(bf16[1024,384]{1,0:T(8,128)(2,1)} %x_hbm.1, bf16[384,1536]{1,0:T(8,128)(2,1)} %w1_hbm.1, bf16[1536,384]{1,0:T(8,128)(2,1)} %w2_hbm.1, bf16[10,2,384]{2,1,0:T(2,128)(2,1)} %bitcast.3, s32[2,1024]{1,0:T(2,128)} %lab_hbm.1, s32[2,1024]{1,0:T(2,128)} %mask_hbm.1, ...), custom_call_target="tpu_custom_call" | custom-call | tf_op jit(solution)/shard_map/step/pallas_call | solution.py:433
  56.5 1.9 %combine.1 = (f32[2]{0:T(128)}, f32[144,128]{1,0:T(8,128)}, f32[144,128]{1,0:T(8,128)}) custom-call(f32[1,128]{1,0:T(1,128)} %get-tuple-element.9.gram_hbm, f32[2,144,128]{2,1,0:T(8,128)} %get-tuple-element.10.gin_hbm, f32[2,144,128]{2,1,0:T(8,128)} %get-tuple-element.11.gout_hbm), custom_call_target="tpu_custom_call" | custom-call | tf_op jit(solution)/shard_map/combine/pallas_call | solution.py:443

commit v9 on v7

--- a/solution.py
+++ b/solution.py
@@ -434,7 +434,7 @@
             out_specs=[hbm, hbm, vmem],
             scratch_shapes=scratch,
             compiler_params=pltpu.CompilerParams(collective_id=0, has_side_effects=True,
-                                                 vmem_limit_bytes=66_900_000),
+                                                 vmem_limit_bytes=56547000),
             name="step",
         )(*args)
         weights, grad_in, grad_out = pl.pallas_call(
@@ -443,7 +443,7 @@
             in_specs=[vmem, hbm, hbm],
             out_specs=[pl.BlockSpec(memory_space=pltpu.SMEM), vmem, vmem],
             scratch_shapes=[pltpu.VMEM(outs[0].shape, F32), pltpu.VMEM(outs[1].shape, F32), dma((2,))],
-            compiler_params=pltpu.CompilerParams(vmem_limit_bytes=66_900_000),
+            compiler_params=pltpu.CompilerParams(vmem_limit_bytes=56547000),
             name="combine",
         )(gram, gin, gout)
         return weights, grad_in.reshape(-1), grad_out.reshape(-1)

time: 59.2 us -> 57.9 us (0.978)
  Pallas kernels: 58.2 us -> 57 us
    pallas_call x1, Pallas kernels: 2.35 us -> 1.67 us  [local_step(): pl.pallas_call(combine, out_shape=[jax.ShapeDtypeStruct((TASKS,), F32), p...]
where the time goes in v9:
time: 57.9 us; the launch traced here: 57.8 us
  Pallas kernels  57 us (98%)
  between operations  0.8 us (1%)
    pallas_call x1, Pallas kernels, local_step(): pl.pallas_call(kernel, out_shape=outs, in_specs=[hbm] * len(args), out_sp...  55.3 us
    pallas_call x1, Pallas kernels, local_step(): pl.pallas_call(combine, out_shape=[jax.ShapeDtypeStruct((TASKS,), F32), p...  1.67 us

profile of v9, /device:TPU:0, one launch (start us, length us, event | category | flops | bytes accessed | tf_op | source)
XLA Modules:
  0.0 57.8 jit_solution(13569865663672374382)
XLA Ops:
  0.6 55.3 %step.1 = (f32[2,144,128]{2,1,0:T(8,128)}, f32[2,144,128]{2,1,0:T(8,128)}, f32[1,128]{1,0:T(1,128)S(1)}) custom-call(bf16[1024,384]{1,0:T(8,128)(2,1)} %x_hbm.1, bf16[384,1536]{1,0:T(8,128)(2,1)} %w1_hbm.1, bf16[1536,384]{1,0:T(8,128)(2,1)} %w2_hbm.1, bf16[10,2,384]{2,1,0:T(2,128)(2,1)} %bitcast.3, s32[2,1024]{1,0:T(2,128)} %lab_hbm.1, s32[2,1024]{1,0:T(2,128)} %mask_hbm.1, ...), custom_call_target="tpu_custom_call" | custom-call | tf_op jit(solution)/shard_map/step/pallas_call | solution.py:430
  55.9 1.7 %combine.1 = (f32[2]{0:T(128)}, f32[144,128]{1,0:T(8,128)}, f32[144,128]{1,0:T(8,128)}) custom-call(f32[1,128]{1,0:T(1,128)S(1)} %get-tuple-element.9.gram_ref, f32[2,144,128]{2,1,0:T(8,128)} %get-tuple-element.10.gin_hbm, f32[2,144,128]{2,1,0:T(8,128)} %get-tuple-element.11.gout_hbm), custom_call_target="tpu_custom_call" | custom-call | tf_op jit(solution)/shard_map/combine/pallas_call | solution.py:440

commit v10 on v9

--- a/solution.py
+++ b/solution.py
@@ -194,14 +194,17 @@
         heads = jnp.concatenate([heads_ref[:, 0, :], pad, heads_ref[:, 1, :], pad], axis=0)
         logits = dot(heads, zt, ((1,), (0,)))
         cls = lax.broadcasted_iota(jnp.int32, (16, TOK), 0)
-        for t in range(TASKS):
-            score = jnp.where(cls < CLS, logits[16 * t:16 * (t + 1)], -jnp.inf)
-            ex = jnp.exp(score - jnp.max(score, axis=0, keepdims=True))
-            prob = ex / jnp.sum(ex, axis=0, keepdims=True)
-            onehot = jnp.where(lab_ref[t:t + 1, :] == cls, 1.0, 0.0)
-            err_ref[t] = (mask_ref[t:t + 1, :].astype(F32) * (prob - onehot)).astype(BF16)
-            head = heads[16 * t:16 * (t + 1)]
-            dz_ref[:, t * DIM:(t + 1) * DIM] = dot(err_ref[t], head, ((0,), (0,))).astype(BF16)
+
+    def classes(t):
+        score = jnp.where(cls < CLS, logits[16 * t:16 * (t + 1)], -jnp.inf)
+        ex = jnp.exp(score - jnp.max(score, axis=0, keepdims=True))
+        prob = ex / jnp.sum(ex, axis=0, keepdims=True)
+        onehot = jnp.where(lab_ref[t:t + 1, :] == cls, 1.0, 0.0)
+        err_ref[t] = (mask_ref[t:t + 1, :].astype(F32) * (prob - onehot)).astype(BF16)
+        head = heads[16 * t:16 * (t + 1)]
+        dz_ref[:, t * DIM:(t + 1) * DIM] = dot(err_ref[t], head, ((0,), (0,))).astype(BF16)
+
+    classes(0)
 
     inv = []
 
@@ -300,6 +303,7 @@
 
     compute_b(0, 0)
     start(Y[0])
+    classes(1)
     compute_b(0, 1)
     start(X[0])
     compute_b(1, 1)

time: 57.9 us -> 58 us (level)
  no operation moved by 1% of the time
where the time goes in v10:
time: 58 us; the launch traced here: 57.8 us
  Pallas kernels  57 us (98%)
  between operations  0.8 us (1%)
    pallas_call x1, Pallas kernels, local_step(): pl.pallas_call(kernel, out_shape=outs, in_specs=[hbm] * len(args), out_sp...  55.3 us
    pallas_call x1, Pallas kernels, local_step(): pl.pallas_call(combine, out_shape=[jax.ShapeDtypeStruct((TASKS,), F32), p...  1.67 us

profile of v10, /device:TPU:0, one launch (start us, length us, event | category | flops | bytes accessed | tf_op | source)
XLA Modules:
  0.0 57.8 jit_solution(11358167352299699390)
XLA Ops:
  0.6 55.3 %step.1 = (f32[2,144,128]{2,1,0:T(8,128)}, f32[2,144,128]{2,1,0:T(8,128)}, f32[1,128]{1,0:T(1,128)S(1)}) custom-call(bf16[1024,384]{1,0:T(8,128)(2,1)} %x_hbm.1, bf16[384,1536]{1,0:T(8,128)(2,1)} %w1_hbm.1, bf16[1536,384]{1,0:T(8,128)(2,1)} %w2_hbm.1, bf16[10,2,384]{2,1,0:T(2,128)(2,1)} %bitcast.3, s32[2,1024]{1,0:T(2,128)} %lab_hbm.1, s32[2,1024]{1,0:T(2,128)} %mask_hbm.1, ...), custom_call_target="tpu_custom_call" | custom-call | tf_op jit(solution)/shard_map/step/pallas_call | solution.py:434
  56.0 1.7 %combine.1 = (f32[2]{0:T(128)}, f32[144,128]{1,0:T(8,128)}, f32[144,128]{1,0:T(8,128)}) custom-call(f32[1,128]{1,0:T(1,128)S(1)} %get-tuple-element.9.gram_ref, f32[2,144,128]{2,1,0:T(8,128)} %get-tuple-element.10.gin_hbm, f32[2,144,128]{2,1,0:T(8,128)} %get-tuple-element.11.gout_hbm), custom_call_target="tpu_custom_call" | custom-call | tf_op jit(solution)/shard_map/combine/pallas_call | solution.py:444
